TPU v7x, 256 devices: a 4x2x16 block of a 4x16x16 slice. The times are simulated.
256 devices in a mesh: grp: 2 (over y), aux: 16 (over z), orb: 4 (over x), occ: 2 (over core).
Axes of the slice: x: 4, y: 2, z: 16, core: 2. Of those that a mesh axis runs over, the one named last changes fastest.
The devices are a block of a 4x16x16 slice.
Arguments:
- b_tiles: bfloat16 [256, 32, 4, 128, 128], P(('grp', 'aux'), 'orb'), parts along dimension 0, may hold values from -0.25 to 0.25
- nu_block: int32 [256, 32, 4], P(('grp', 'aux'), 'orb'), parts along dimension 0, may hold values from 0 to 31
- tile_mask: int32 [256, 32, 4], P(('grp', 'aux'), 'orb'), parts along dimension 0, may hold values 0 or 1
- assignment: int32 [256], P(('grp', 'aux')), parts along dimension 0, may hold values from 0 to 127, each once
- metric_factor: float32 [256], P('grp'), parts along dimension 0, may hold values from 0.05 to 0.3
- orbitals: bfloat16 [800, 4000], P('grp'), parts along dimension 0, may hold values from -6 to 6
- occupied_index: int32 [64], P(('grp', 'occ')), parts along dimension 0, may hold values from 0 to 399
Outputs:
- exchange: float32 [8192, 4096], P(('grp', 'aux', 'occ'), 'orb'), parts along dimension 0
There are 2 independent parts, one for each index of `grp`. A program takes and returns all parts, laid end to end along the dimension named above; each array names one. Nothing has to cross between parts.
Inputs may be any that keep to these rules, and one draw needn't show every extreme that they name: `nu_block`: each entry names a column block. `assignment`: each number once. `occupied_index`: repeats may occur.
All inputs are finite; a program needn't handle non-finite values. No bound on the sum of `tile_mask` on one device may be relied on, other than what follows from the above.
Results may differ from a plain program's by a relative error of at most 0.0033.
Values may be sent and summed in bfloat16 or wider, within the bound.
No kernel may reach another device: no remote copies, remote signals or barrier semaphores. Data moves between devices by JAX's collectives and lax.ppermute only.
A program may use at most 128 MiB of HBM per device.

v0:
```python
import jax
import jax.numpy as jnp
from jax import lax
from jax.sharding import PartitionSpec as P


def picked_2(x, axis, root):
    return lax.dynamic_index_in_dim(lax.all_gather(x, axis), root, 0, keepdims=False)


def per_device(b_tiles, nu_block, tile_mask, assignment, metric_factor, orbitals, occupied_index):
    naux_dev = b_tiles.shape[0]
    row_blocks = b_tiles.shape[1]
    tile_size = b_tiles.shape[3]
    n_basis = orbitals.shape[1]
    nblocks = (n_basis + tile_size - 1) // tile_size
    padded = nblocks * tile_size
    mu_dev = row_blocks * tile_size
    batch_dev = occupied_index.shape[0]
    picked = jnp.take(orbitals, occupied_index, axis=0)
    picked = jnp.pad(picked, ((0, 0), (0, padded - n_basis)))
    blocks = picked.reshape(batch_dev, nblocks, tile_size)
    chosen = blocks[:, nu_block] * tile_mask.astype(jnp.bfloat16)[None, :, :, :, None]
    half_product = jnp.einsum(
        "pmsab,ipmsb->pima", b_tiles, chosen, preferred_element_type=jnp.float32
    )
    half_product = half_product.reshape(naux_dev, batch_dev, mu_dev)
    lookup_table = (
        assignment[:, None] == jnp.arange(metric_factor.shape[0], dtype=jnp.int32)[None, :]
    ).astype(jnp.float32)
    factors = jnp.dot(lookup_table, metric_factor, precision=lax.Precision.HIGHEST)
    row_index = lax.axis_index("orb") * mu_dev + jnp.arange(mu_dev, dtype=jnp.int32)
    scaled_slab = jnp.where(
        row_index[None, None, :] < n_basis, half_product * factors[:, None, None], 0.0
    )
    half_slab = scaled_slab.astype(jnp.bfloat16).reshape(naux_dev * batch_dev, mu_dev)
    block_rows = padded // (lax.axis_size("aux") * lax.axis_size("occ"))
    everyone = lax.all_gather(half_slab, ("aux", "occ"), axis=0, tiled=True)
    group_index = lax.axis_index("aux") * lax.axis_size("occ") + lax.axis_index("occ")
    first_row = group_index * block_rows
    root_index = first_row // mu_dev
    row_offset = first_row - root_index * mu_dev
    owner_slice = lax.dynamic_slice_in_dim(everyone, row_offset, block_rows, 1)
    gathered_owner = picked_2(owner_slice, "orb", root_index)
    owned_tile = lax.dot_general(
        gathered_owner, everyone, (((0,), (0,)), ((), ())), preferred_element_type=jnp.float32
    )
    return owned_tile


def solution(mesh):
    in_specs = (
        P(("grp", "aux"), "orb", None, None, None),
        P(("grp", "aux"), "orb", None),
        P(("grp", "aux"), "orb", None),
        P(("grp", "aux")),
        P("grp"),
        P("grp", None),
        P(("grp", "occ")),
    )
    out_specs = P(("grp", "aux", "occ"), "orb")
    return jax.shard_map(
        per_device, mesh=mesh, in_specs=in_specs, out_specs=out_specs, check_vma=False
    )
```

profile of v0, /device:TPU:33, one launch (start us, length us, event | category | flops | bytes accessed | tf_op | source)
XLA Modules:
  0.0 178.4 jit_solution(16558601712163441138)
XLA Ops:
  6.5 0.0 copy-start
  6.6 0.0 all-gather.4.cloned.1.call-start
  6.6 0.8 compare_and_fusion
  7.4 0.8 compare_select_fusion.1
  8.2 0.9 convolution_bitcast_fusion.1
  9.1 0.1 mul.36
  9.1 0.1 mul.37
  9.2 0.7 convert_element_type.10
  10.0 0.1 copy.12
  10.1 0.7 compare_select_fusion
  10.8 0.1 copy.10
  10.9 0.1 reshape.35
  11.1 0.0 copy-done
  11.1 0.6 gather_fusion
  11.7 0.1 broadcast_select_fusion
  11.8 1.8 gather_fusion.1
  13.6 6.0 %convolution_bitcast_fusion = f32[8,16,8,128]{3,1,2,0:T(8,128)S(1)} fusion(bf16[8,8,4,128,128]{4,3,2,1,0:T(8,128)(2,1)} %param.7, bf16[8,8,4,16,128]{4,3,2,1,0:T(8,128)(2,1)} %bitcast.33, bf16[8,8,4]{2,1,0:T(8,128)(2,1)S(1)} %copy.12), kind=kOutput, calls=%fused_computation.2 | convolution fusion | flops 134742016 | bytes 9961984 | tf_op jit(solution)/shard_map/pmsab,ipmsb->pima/dot_general | solution.py:24
  19.6 0.2 copy.13
  19.8 0.9 fusion.6
  20.7 0.1 all-gather.4.cloned.1.call-update
  20.8 0.1 all-gather.6.cloned.1.call-start
  20.9 92.2 %all-gather.4.cloned.1.call-done = bf16[4096,1024]{1,0:T(8,128)(2,1)} async-done(((bf16[128,1024]{1,0:T(8,128)(2,1)}), bf16[4096,1024]{1,0:T(8,128)(2,1)}) %all-gather.4.cloned.1.call-update) | async-done | bytes 8388624 | tf_op jit(solution)/shard_map/all_gather | solution.py:38
  113.0 2.3 %constant_dynamic-slice_fusion = bf16[4096,128]{1,0:T(8,128)(2,1)} fusion(bf16[4096,1024]{1,0:T(8,128)(2,1)} %all-gather.4.cloned.1.call-done, s32[]{:T(128)S(6)} %select_n.34), kind=kLoop, calls=%fused_computation.25 | loop fusion | bytes 2097156 | tf_op jit(solution)/shard_map/dynamic_slice | solution.py:43
  115.4 0.1 all-gather.6.cloned.1.call-update
  115.4 50.4 %all-gather.6.cloned.1.call-done = bf16[16384,128]{1,0:T(8,128)(2,1)} async-done(((bf16[4096,128]{1,0:T(8,128)(2,1)}), bf16[16384,128]{1,0:T(8,128)(2,1)}) %all-gather.6.cloned.1.call-update) | async-done | bytes 4194320 | tf_op jit(solution)/shard_map/all_gather | solution.py:8
  165.8 5.8 %fusion = f32[128,1024]{1,0:T(8,128)} fusion(bf16[4096,1024]{1,0:T(8,128)(2,1)} %all-gather.4.cloned.1.call-done, bf16[4,4096,128]{2,1,0:T(8,128)(2,1)} %bitcast.35, s32[]{:T(128)S(6)} %select_n.35), kind=kOutput, calls=%fused_computation.4 | convolution fusion | flops 1073741824 | bytes 9961476 | tf_op jit(solution)/shard_map/dot_general | solution.py:45
  (4 shorter events, 0.0 us)
Async XLA Ops:
  6.5 4.5 %copy-start = (bf16[400,4000]{1,0:T(8,128)(2,1)S(1)}, bf16[400,4000]{1,0:T(8,128)(2,1)}, u32[]{:S(2)}) copy-start(bf16[400,4000]{1,0:T(8,128)(2,1)} %param.12) | copy-start | bytes 9600004
  6.6 106.5 %all-gather.4.cloned.1.call-start = ((), (), s32[]{:S(2)}) async-start(), calls=%async_computation | async-start | bytes 8650752 | tf_op jit(solution)/shard_map/all_gather | solution.py:38
  20.8 145.0 %all-gather.6.cloned.1.call-start = ((), (), s32[]{:S(2)}) async-start(), calls=%async_computation.1 | async-start | bytes 5242880 | tf_op jit(solution)/shard_map/all_gather | solution.py:8
Sparse Core Ops, SparseCore 0:
  20.9 92.0 all-gather.3
  115.5 50.2 all-gather.5
where the time goes:
time: 179 us; the launch traced here: 178 us
  waiting for transfers between devices  143 us (80%)
  between operations  13.5 us (8%)
  matrix products  12.7 us (7%)
  local copies, waits for them, and re-layouts  5.45 us (3%)
  other arithmetic  4.1 us (2%)
    all_gather x1, waiting for transfers between devices, per_device(): everyone = lax.all_gather(half_slab, ('aux', 'occ'), axis=0, tiled=True)  92.2 us
    all_gather x1, waiting for transfers between devices, picked_2(): lax.all_gather(x, axis)  50.4 us
    dot_general x1, matrix products, per_device(): jnp.einsum('pmsab,ipmsb->pima', b_tiles, chosen, preferred_element_type=j...  6.04 us
    dot_general x1, matrix products, per_device(): lax.dot_general(gathered_owner, everyone, (((0,), (0,)), ((), ())), prefe...  5.79 us
  transfers between devices with their start and end apart: 2, of which 2 were waited for; matrix products, arithmetic and copies ran while one was open for 0% of the time, Pallas kernels for 0%

commit v1 on v0

v1 whole, which is shorter than its diff:
```python
import functools

import jax
import jax.numpy as jnp
from jax import lax
from jax.experimental import pallas as pl
from jax.experimental.pallas import tpu as pltpu
from jax.sharding import PartitionSpec as P


VMEM_BYTES = 12 * 1024 * 1024
TRANSFORM_VMEM_BYTES = 60 * 1024 * 1024
STAGE_FLOPS = 2_000_000_000


def contract_last(left, right):
    return lax.dot_general(
        left, right, (((1,), (1,)), ((), ())), preferred_element_type=jnp.float32
    )


def transform_kernel(
    build, n_basis, block0, place_ref, index_ref, nu_ref, mask_ref, assign_ref, metric_ref,
    table_or_orbitals_ref, tiles_ref, out_ref, *rest
):
    n_p, _, slots, tile, _ = tiles_ref.shape
    lanes = out_ref.shape[1]
    n_i = lanes // n_p
    step = pl.program_id(0)
    if build:
        table_ref, lane_mask_ref, rows_ref, sem = rest
    else:
        table_ref = table_or_orbitals_ref
        (lane_mask_ref,) = rest
    blocks = table_ref.shape[0] // tile - 1

    @pl.when(step == 0)
    def _():
        lane = lax.broadcasted_iota(jnp.int32, (16, lanes), 1)
        for p in range(n_p):
            lane_mask_ref[p] = jnp.where(lane // n_i == p, 1.0, 0.0).astype(jnp.bfloat16)
        if build:
            group = rows_ref.shape[1]
            for i in range(n_i):
                at = pl.ds(pl.multiple_of(index_ref[i] // group * group, group), group)
                pltpu.make_async_copy(
                    table_or_orbitals_ref.at[at, :], rows_ref.at[i], sem.at[i]
                ).start()
            row = lax.broadcasted_iota(jnp.int32, (n_i * group, lanes), 0)
            col = lax.broadcasted_iota(jnp.int32, (n_i * group, lanes), 1)
            wanted = jnp.zeros((n_i * group, lanes), jnp.int32)
            for i in range(n_i):
                wanted = jnp.where(col % n_i == i, i * group + index_ref[i] % group, wanted)
            one_hot = jnp.where(row == wanted, 1.0, 0.0).astype(jnp.bfloat16)
            for i in range(n_i):
                pltpu.make_async_copy(
                    table_or_orbitals_ref.at[pl.ds(0, group), :], rows_ref.at[i], sem.at[i]
                ).wait()
            table_ref[pl.ds((blocks - 1) * tile, 2 * tile), :] = jnp.zeros(
                (2 * tile, lanes), jnp.bfloat16
            )
            for k in range(blocks):
                wide = min(tile, n_basis - k * tile)
                got = rows_ref[:, :, k * tile : k * tile + wide].reshape(n_i * group, wide)
                turned = lax.dot_general(
                    got, one_hot, (((0,), (0,)), ((), ())), preferred_element_type=jnp.float32
                )
                table_ref[k * tile : k * tile + wide, :] = turned.astype(jnp.bfloat16)

    total = jnp.zeros((tile, lanes), jnp.float32)
    for p in range(n_p):
        lane_mask = lane_mask_ref[p]
        for s in range(0, slots, 2):
            weights = []
            for t in (s, s + 1):
                nu = jnp.where(mask_ref[p, t, block0 + step] > 0, nu_ref[p, t, block0 + step], blocks)
                part = table_ref[pl.ds(pl.multiple_of(nu * tile, tile), tile), :]
                part = part.reshape(tile // 16, 16, lanes) * lane_mask[None]
                weights.append(part.reshape(tile, lanes))
            left = jnp.concatenate([tiles_ref[p, 0, s], tiles_ref[p, 0, s + 1]], axis=1)
            total = total + jnp.dot(
                left, jnp.concatenate(weights, axis=0), preferred_element_type=jnp.float32
            )
    lane = lax.broadcasted_iota(jnp.int32, (1, lanes), 1)
    factors = jnp.zeros((1, lanes), jnp.float32)
    for p in range(n_p):
        factors = jnp.where(lane // n_i == p, metric_ref[assign_ref[p]], factors)
    row = place_ref[2] + (block0 + step) * tile + lax.broadcasted_iota(jnp.int32, (tile, lanes), 0)
    out_ref[...] = jnp.where(row < n_basis, total * factors, 0.0).astype(out_ref.dtype)


def transform(build, block0, n_blocks, n_basis, scalars, table, b_tiles):
    n_p, _, slots, tile, _ = b_tiles.shape
    n_i = scalars[1].shape[0]
    lanes = n_p * n_i
    blocks = (n_basis + tile - 1) // tile
    smem = pl.BlockSpec(memory_space=pltpu.SMEM)
    vmem = pl.BlockSpec(memory_space=pltpu.VMEM)
    table_shape = jax.ShapeDtypeStruct(((blocks + 1) * tile, lanes), jnp.bfloat16)
    out_shape = [jax.ShapeDtypeStruct((n_blocks * tile, lanes), jnp.bfloat16)]
    out_specs = [pl.BlockSpec((tile, lanes), lambda m: (m, 0))]
    scratch = [pltpu.VMEM((n_p, 16, lanes), jnp.bfloat16)]
    if build:
        out_shape.append(table_shape)
        out_specs.append(vmem)
        scratch += [
            pltpu.VMEM((n_i, 8, n_basis), jnp.bfloat16),
            pltpu.SemaphoreType.DMA((n_i,)),
        ]
    return pl.pallas_call(
        functools.partial(transform_kernel, build, n_basis, block0),
        grid=(n_blocks,),
        out_shape=out_shape,
        in_specs=[smem] * len(scalars)
        + [pl.BlockSpec(memory_space=pl.ANY) if build else vmem]
        + [pl.BlockSpec((n_p, 1, slots, tile, tile), lambda m: (0, block0 + m, 0, 0, 0))],
        out_specs=out_specs,
        scratch_shapes=scratch,
        compiler_params=pltpu.CompilerParams(vmem_limit_bytes=TRANSFORM_VMEM_BYTES),
        cost_estimate=pl.CostEstimate(
            flops=2 * n_blocks * n_p * slots * tile * tile * lanes,
            bytes_accessed=2 * n_blocks * n_p * slots * tile * tile,
            transcendentals=0,
        ),
        name="transform_first" if build else "transform_rest",
    )(*scalars, table, b_tiles)


def stage_kernel(place_ref, *refs):
    *halves, came, out_ref = refs
    count = out_ref.shape[0] // 2

    @pl.when(place_ref[0] == 0)
    def _():
        at = pl.ds(pl.multiple_of(place_ref[3], count), count)
        for k in range(2):
            low, high = halves[2 * k], halves[2 * k + 1]

            @pl.when(place_ref[4] == 0)
            def _():
                out_ref[k * count : (k + 1) * count, :] = low[at, :]

            @pl.when(place_ref[4] != 0)
            def _():
                out_ref[k * count : (k + 1) * count, :] = high[at, :]

    @pl.when(place_ref[0] != 0)
    def _():
        out_ref[...] = came[...]


def stage(place, pair, came, rows):
    vmem = pl.BlockSpec(memory_space=pltpu.VMEM)
    operands = [h for s in pair for h in s] + [came]
    return pl.pallas_call(
        stage_kernel,
        out_shape=jax.ShapeDtypeStruct((2 * rows, pair[0][0].shape[1]), pair[0][0].dtype),
        in_specs=[pl.BlockSpec(memory_space=pltpu.SMEM)] + [vmem] * len(operands),
        out_specs=vmem,
        compiler_params=pltpu.CompilerParams(vmem_limit_bytes=VMEM_BYTES),
        cost_estimate=pl.CostEstimate(flops=STAGE_FLOPS, bytes_accessed=0, transcendentals=0),
        name="stage",
    )(place, *operands)


def accumulate_kernel(n, has_prev, place_ref, *refs):
    pairs = [refs[8 * j : 8 * j + 8] for j in range(n)]
    rest = refs[8 * n :]
    prev, outs = (rest[:2], rest[2:]) if has_prev else (None, rest)
    link, core = place_ref[0], place_ref[1]
    mine = outs[0].shape[0]
    rows = []
    for j in range(n):
        both = []
        for side in range(2):
            which = core if side == 0 else 1 - core
            cut = []
            for k in range(2):
                at = pl.ds(pl.multiple_of(k * 2 * mine + which * mine, mine), mine)
                c = [r[at, :] for r in pairs[j][:4]]
                cut.append(
                    jnp.where(
                        link < 2, jnp.where(link == 0, c[0], c[1]), jnp.where(link == 2, c[2], c[3])
                    )
                )
            both.append(jnp.concatenate(cut, axis=1))
        rows.append(both)
    half = pairs[0][4].shape[0]
    step = 256
    for h in range(2):
        for c in range(half // step):
            cut = slice(c * step, (c + 1) * step)
            right = [jnp.concatenate([p[4 + h][cut, :], p[6 + h][cut, :]], axis=1) for p in pairs]
            for side in range(2):
                at = pl.ds(h * half + c * step, step)
                acc = prev[side][:, at] if has_prev else None
                for j in range(n):
                    part = contract_last(rows[j][side], right[j])
                    acc = part if acc is None else acc + part
                outs[side][:, at] = acc


def accumulate(place, candidates, pairs, prev, block_rows, columns):
    n = len(pairs)
    has_prev = prev is not None
    operands = []
    for c, pair in zip(candidates, pairs, strict=True):
        operands += list(c) + [pair[0][0], pair[0][1], pair[1][0], pair[1][1]]
    operands += list(prev) if has_prev else []
    vmem = pl.BlockSpec(memory_space=pltpu.VMEM)
    flops = 2 * 2 * block_rows * columns * 2 * n * pairs[0][0][0].shape[1]
    return pl.pallas_call(
        functools.partial(accumulate_kernel, n, has_prev),
        out_shape=[jax.ShapeDtypeStruct((block_rows, columns), jnp.float32)] * 2,
        in_specs=[pl.BlockSpec(memory_space=pltpu.SMEM)] + [vmem] * len(operands),
        out_specs=[vmem] * 2,
        compiler_params=pltpu.CompilerParams(vmem_limit_bytes=VMEM_BYTES),
        cost_estimate=pl.CostEstimate(flops=flops, bytes_accessed=0, transcendentals=0),
        name="accumulate",
    )(place, *operands)


def per_device(b_tiles, nu_block, tile_mask, assignment, metric_factor, orbitals, occupied_index):
    row_blocks, tile_size = b_tiles.shape[1], b_tiles.shape[3]
    n_basis = orbitals.shape[1]
    padded = (n_basis + tile_size - 1) // tile_size * tile_size
    mu_dev = row_blocks * tile_size
    n_aux, n_orb, n_occ = lax.axis_size("aux"), lax.axis_size("orb"), lax.axis_size("occ")
    z, x, core = lax.axis_index("aux"), lax.axis_index("orb"), lax.axis_index("occ")
    block_rows = padded // (n_aux * n_occ)
    plane_rows = block_rows * n_occ
    per_orb = mu_dev // plane_rows
    half = mu_dev // 2
    per_half = half // plane_rows

    root = z // per_orb
    away = x - root
    link = lax.rem(jnp.where(core == 0, away, -away) + n_orb, n_orb)
    in_half = lax.rem(z, per_half) * plane_rows
    upper = lax.rem(z, per_orb) // per_half
    place = jnp.stack([link, core, x * mu_dev, in_half, upper]).astype(jnp.int32)

    scalars = (
        place,
        occupied_index,
        nu_block.transpose(0, 2, 1),
        tile_mask.transpose(0, 2, 1),
        assignment,
        metric_factor,
    )
    low, table = transform(True, 0, row_blocks // 2, n_basis, scalars, orbitals, b_tiles)
    (high,) = transform(False, row_blocks // 2, row_blocks // 2, n_basis, scalars, table, b_tiles)

    swap = [(0, 1), (1, 0)]
    a = (low, high)
    b = tuple(lax.ppermute(h, "occ", swap) for h in a)
    ring = [(2 * i, 2 * ((i + 1) % n_aux)) for i in range(n_aux)]
    ring += [(2 * i + 1, 2 * ((i - 1) % n_aux) + 1) for i in range(n_aux)]

    def forward(pair):
        got = []
        for k in range(2):
            got.append(lax.ppermute(pair[k], ("aux", "occ"), ring))
        return tuple(got)

    def along(payload, links):
        pairs = []
        for i in range(n_aux):
            for c, sign in ((0, 1), (1, -1)):
                for source, target in links:
                    at = [(i * n_orb + (i // per_orb + sign * k) % n_orb) * 2 + c for k in (source, target)]
                    pairs.append(tuple(at))
        return lax.ppermute(payload, ("aux", "orb", "occ"), pairs)

    chain = [(k, k + 1) for k in range(n_orb - 1)]
    steps = n_aux // 2
    pairs, payloads = [], []
    came = jnp.zeros((2 * plane_rows, low.shape[1]), low.dtype)
    held = a
    for t in range(1, steps + 1):
        a = forward(a)
        pair = (held, a)
        pairs.append(pair)
        if t < steps:
            b = forward(b)
            held = b
        payloads.append(stage(place, pair, came, plane_rows))
        came = along(payloads[-1], chain)
    payloads.append(came)
    n = len(pairs)
    candidates = [payloads[j : j + 4] for j in range(n - 2)]
    two, one = payloads[n - 2], payloads[n - 1]
    candidates.append([two, one, came, along(two, [(0, 3)])])
    candidates.append([one, came, along(one, [(0, 2)]), along(one, [(0, 3)])])

    partial = None
    for lo, hi in ((0, n - 4), (n - 4, n - 3), (n - 3, n)):
        partial = accumulate(place, candidates[lo:hi], pairs[lo:hi], partial, block_rows, mu_dev)
    mine, other = partial
    return mine + lax.ppermute(other, "occ", swap)


def solution(mesh):
    in_specs = (
        P(("grp", "aux"), "orb", None, None, None),
        P(("grp", "aux"), "orb", None),
        P(("grp", "aux"), "orb", None),
        P(("grp", "aux")),
        P("grp"),
        P("grp", None),
        P(("grp", "occ")),
    )
    out_specs = P(("grp", "aux", "occ"), "orb")

    return jax.shard_map(
        per_device, mesh=mesh, in_specs=in_specs, out_specs=out_specs, check_vma=False
    )
```

time: 179 us -> 155 us (0.87)
  waiting for transfers between devices: 143 us -> 56.2 us
  starting transfers between devices: 0.07 us -> 73.3 us
  Pallas kernels: 0 us -> 21.4 us
  between operations: 13.5 us -> 0.53 us
  matrix products: 12.7 us -> 0 us
  local copies, waits for them, and re-layouts: 5.45 us -> 1.61 us
  other arithmetic: 4.1 us -> 0.87 us
    all_gather x2 -> x0, waiting for transfers between devices: 143 us -> none  [the longest x1 92.2 us: per_device(): everyone = lax.all_gather(half_slab, ('aux', 'occ'), axis=0, tiled=True)]
    ppermute x0 -> x44, starting transfers between devices: none -> 73.3 us  [the longest x11 34.2 us: along(): return lax.ppermute(payload, ('aux', 'orb', 'occ'), pairs)]
    ppermute x0 -> x44, waiting for transfers between devices: none -> 56.2 us  [the longest x30 45.6 us: forward(): got.append(lax.ppermute(pair[k], ('aux', 'occ'), ring))]
    pallas_call x0 -> x13, Pallas kernels: none -> 21.4 us  [the longest x2 11.9 us: transform(): pl.pallas_call(functools.partial(transform_kernel, build, n_basis, block0...]
    dot_general x3 -> x0, matrix products: 12.7 us -> none  [the longest x1 6.04 us: per_device(): jnp.einsum('pmsab,ipmsb->pima', b_tiles, chosen, preferred_element_type=j...]
    gather x2 -> x0, local copies, waits for them, and re-layouts: 2.39 us -> none  [the longest x1 1.76 us: per_device(): blocks[:, nu_block] * tile_mask.astype(jnp.bfloat16)[None, :, :, :, None]]
    dynamic_slice x1 -> x0, local copies, waits for them, and re-layouts: 2.33 us -> none  [per_device(): owner_slice = lax.dynamic_slice_in_dim(everyone, row_offset, block_rows, 1)]
  transfers between devices with their start and end apart: 2 -> 44, of which waited for: 2 -> 38; matrix products, arithmetic and copies ran while one was open for 0% -> 0% of each run, Pallas kernels for 0% -> 3%
where the time goes in v1:
time: 155 us; the launch traced here: 154 us
  starting transfers between devices  73.3 us (47%)
  waiting for transfers between devices  56.2 us (36%)
  Pallas kernels  21.4 us (14%)
  local copies, waits for them, and re-layouts  1.61 us (1%)
    ppermute x30, waiting for transfers between devices, forward(): got.append(lax.ppermute(pair[k], ('aux', 'occ'), ring))  45.6 us
    ppermute x11, starting transfers between devices, along(): return lax.ppermute(payload, ('aux', 'orb', 'occ'), pairs)  34.2 us
    ppermute x30, starting transfers between devices, forward(): got.append(lax.ppermute(pair[k], ('aux', 'occ'), ring))  27.1 us
    pallas_call x2, Pallas kernels, transform(): pl.pallas_call(functools.partial(transform_kernel, build, n_basis, block0...  11.9 us
    ppermute x1, starting transfers between devices, per_device(): return mine + lax.ppermute(other, 'occ', swap)  11.5 us
    ppermute x11, waiting for transfers between devices, along(): return lax.ppermute(payload, ('aux', 'orb', 'occ'), pairs)  9.13 us
    pallas_call x3, Pallas kernels, accumulate(): pl.pallas_call(functools.partial(accumulate_kernel, n, has_prev), out_sha...  4.8 us
    pallas_call x8, Pallas kernels, stage(): pl.pallas_call(stage_kernel, out_shape=jax.ShapeDtypeStruct((2 * rows, pa...  4.72 us
  transfers between devices with their start and end apart: 44, of which 38 were waited for; matrix products, arithmetic and copies ran while one was open for 0% of the time, Pallas kernels for 3%

profile of v1, /device:TPU:33, one launch (start us, length us, event | category | flops | bytes accessed | tf_op | source)
XLA Modules:
  0.0 154.0 jit_solution(9803772774261440074)
XLA Ops:
  0.0 0.7 stack.23.place_ref
  0.7 6.8 %transform_first.1 = (bf16[512,128]{1,0:T(8,128)(2,1)}, bf16[4224,128]{1,0:T(8,128)(2,1)}) custom-call(s32[5]{0:T(128)} %stack.23.place_ref, s32[16]{0:T(128)} %index_ref.3, s32[8,4,8]{2,1,0:T(4,128)} %bitcast.7, s32[8,4,8]{2,1,0:T(4,128)} %bitcast.9, s32[8]{0:T(128)} %assign_ref.3, f32[128]{0:T(128)} %metric_ref.3, bf16[400,4000]{1,0:T(8,128)(2,1)} %table_or_orbitals_ref.1, ...), custom_call_target="tpu_custom_call" | custom-call | flops 536870912 | bytes 4194304 | tf_op jit(solution)/shard_map/transform_first/pallas_call | solution.py:110
  7.6 5.1 %transform_rest.1.refs_1_.refs_5_ = bf16[512,128]{1,0:T(8,128)(2,1)} custom-call(s32[5]{0:T(128)} %stack.23.place_ref, s32[16]{0:T(128)} %index_ref.3, s32[8,4,8]{2,1,0:T(4,128)} %bitcast.8, s32[8,4,8]{2,1,0:T(4,128)} %bitcast.10, s32[8]{0:T(128)} %assign_ref.3, f32[128]{0:T(128)} %metric_ref.3, bf16[4224,128]{1,0:T(8,128)(2,1)} %get-tuple-element.14.table_or_orbitals_ref, ...), custom_call_target="tpu_custom_call" | custom-call | flops 536870912 | bytes 4194304 | tf_op jit(solution)/shard_map/transform_rest/pallas_call | solution.py:110
  12.6 22.9 %collective-permute-start.18 = (bf16[512,128]{1,0:T(8,128)(2,1)}, bf16[512,128]{1,0:T(8,128)(2,1)S(1)}, u32[]{:S(2)}, u32[]{:S(2)}) collective-permute-start(bf16[512,128]{1,0:T(8,128)(2,1)} %transform_rest.1.refs_1_.refs_5_), channel_id=1, source_target_pairs={{0,8},{8,16},{16,24},{24,32},{32,40},{40,48},{48,56},{56,64},{64,7... | collective-permute-start | bytes 393224 | tf_op jit(solution)/shard_map/ppermute | solution.py:263
  36.1 1.6 %collective-permute-done.18.refs_3_.refs_7_ = bf16[512,128]{1,0:T(8,128)(2,1)S(1)} collective-permute-done((bf16[512,128]{1,0:T(8,128)(2,1)}, bf16[512,128]{1,0:T(8,128)(2,1)S(1)}, u32[]{:S(2)}, u32[]{:S(2)}) %collective-permute-start.18) | collective-permute-done | bytes 131104 | tf_op jit(solution)/shard_map/ppermute | solution.py:263
  37.8 1.9 %collective-permute-done.12.refs_2_.refs_6_ = bf16[512,128]{1,0:T(8,128)(2,1)S(1)} collective-permute-done((bf16[512,128]{1,0:T(8,128)(2,1)S(1)}, bf16[512,128]{1,0:T(8,128)(2,1)S(1)}, u32[]{:S(2)}, u32[]{:S(2)}) %collective-permute-start.12) | collective-permute-done | bytes 131104 | tf_op jit(solution)/shard_map/ppermute | solution.py:263
  39.7 0.9 copy-done
  41.2 4.8 %collective-permute-start.24 = (bf16[512,128]{1,0:T(8,128)(2,1)S(1)}, bf16[512,128]{1,0:T(8,128)(2,1)S(1)}, u32[]{:S(2)}, u32[]{:S(2)}) collective-permute-start(bf16[512,128]{1,0:T(8,128)(2,1)S(1)} %stage.8.refs_0_), channel_id=1, source_target_pairs={{0,2},{2,4},{4,6},{1,7},{7,5},{5,3},{8,10},{10,12},{12,14},{9,15},... | collective-permute-start | bytes 393224 | tf_op jit(solution)/shard_map/ppermute | solution.py:273
  46.6 1.3 collective-permute-done.24.refs_4_
  47.9 2.0 %collective-permute-done.19.refs_3_.refs_15_ = bf16[512,128]{1,0:T(8,128)(2,1)S(1)} collective-permute-done((bf16[512,128]{1,0:T(8,128)(2,1)S(1)}, bf16[512,128]{1,0:T(8,128)(2,1)S(1)}, u32[]{:S(2)}, u32[]{:S(2)}) %collective-permute-start.19) | collective-permute-done | bytes 131104 | tf_op jit(solution)/shard_map/ppermute | solution.py:263
  49.9 1.7 %collective-permute-done.7.refs_1_.refs_13_ = bf16[512,128]{1,0:T(8,128)(2,1)S(1)} collective-permute-done((bf16[512,128]{1,0:T(8,128)(2,1)S(1)}, bf16[512,128]{1,0:T(8,128)(2,1)S(1)}, u32[]{:S(2)}, u32[]{:S(2)}) %collective-permute-start.7) | collective-permute-done | bytes 131104 | tf_op jit(solution)/shard_map/ppermute | solution.py:263
  51.6 1.4 collective-permute-done.1.refs_0_.refs_12_
  53.0 1.4 collective-permute-done.13.refs_2_.refs_14_
  54.4 0.6 stage.9.refs_1_.refs_8_
  55.0 3.4 %collective-permute-start.25 = (bf16[512,128]{1,0:T(8,128)(2,1)S(1)}, bf16[512,128]{1,0:T(8,128)(2,1)S(1)}, u32[]{:S(2)}, u32[]{:S(2)}) collective-permute-start(bf16[512,128]{1,0:T(8,128)(2,1)S(1)} %stage.9.refs_1_.refs_8_), channel_id=1, source_target_pairs={{0,2},{2,4},{4,6},{1,7},{7,5},{5,3},{8,10},{10,12},{12,14},{9,15},... | collective-permute-start | bytes 393224 | tf_op jit(solution)/shard_map/ppermute | solution.py:273
  59.0 1.4 collective-permute-done.25.refs_4_
  60.4 2.0 %collective-permute-done.20.refs_3_.refs_23_ = bf16[512,128]{1,0:T(8,128)(2,1)S(1)} collective-permute-done((bf16[512,128]{1,0:T(8,128)(2,1)S(1)}, bf16[512,128]{1,0:T(8,128)(2,1)S(1)}, u32[]{:S(2)}, u32[]{:S(2)}) %collective-permute-start.20) | collective-permute-done | bytes 131104 | tf_op jit(solution)/shard_map/ppermute | solution.py:263
  62.4 1.4 collective-permute-done.8.refs_1_.refs_21_
  63.8 1.7 %collective-permute-done.14.refs_2_.refs_22_ = bf16[512,128]{1,0:T(8,128)(2,1)S(1)} collective-permute-done((bf16[512,128]{1,0:T(8,128)(2,1)S(1)}, bf16[512,128]{1,0:T(8,128)(2,1)S(1)}, u32[]{:S(2)}, u32[]{:S(2)}) %collective-permute-start.14) | collective-permute-done | bytes 131104 | tf_op jit(solution)/shard_map/ppermute | solution.py:263
  65.5 1.4 collective-permute-done.2.refs_0_.refs_20_
  66.9 0.6 stage.10.refs_2_.refs_9_.refs_16_
  67.5 2.9 %collective-permute-start.26 = (bf16[512,128]{1,0:T(8,128)(2,1)S(1)}, bf16[512,128]{1,0:T(8,128)(2,1)S(1)}, u32[]{:S(2)}, u32[]{:S(2)}) collective-permute-start(bf16[512,128]{1,0:T(8,128)(2,1)S(1)} %stage.10.refs_2_.refs_9_.refs_16_), channel_id=1, source_target_pairs={{0,2},{2,4},{4,6},{1,7},{7,5},{5,3},{8,10},{10,12},{12,14},{9,15},... | collective-permute-start | bytes 393224 | tf_op jit(solution)/shard_map/ppermute | solution.py:273
  71.2 1.2 collective-permute-done.26.refs_4_
  72.4 2.2 %collective-permute-done.21.refs_3_.refs_31_ = bf16[512,128]{1,0:T(8,128)(2,1)S(1)} collective-permute-done((bf16[512,128]{1,0:T(8,128)(2,1)S(1)}, bf16[512,128]{1,0:T(8,128)(2,1)S(1)}, u32[]{:S(2)}, u32[]{:S(2)}) %collective-permute-start.21) | collective-permute-done | bytes 131104 | tf_op jit(solution)/shard_map/ppermute | solution.py:263
  74.6 1.4 collective-permute-done.9.refs_1_.refs_29_
  76.0 1.4 collective-permute-done.15.refs_2_.refs_30_
  77.4 1.4 collective-permute-done.3.refs_0_.refs_28_
  78.8 0.6 stage.11.refs_3_.refs_10_.refs_17_.refs_24_
  79.4 3.2 %collective-permute-start.27 = (bf16[512,128]{1,0:T(8,128)(2,1)S(1)}, bf16[512,128]{1,0:T(8,128)(2,1)S(1)}, u32[]{:S(2)}, u32[]{:S(2)}) collective-permute-start(bf16[512,128]{1,0:T(8,128)(2,1)S(1)} %stage.11.refs_3_.refs_10_.refs_17_.refs_24_), channel_id=1, source_target_pairs={{0,2},{2,4},{4,6},{1,7},{7,5},{5,3},{8,10},{10,12},{12,14},{9,15},... | collective-permute-start | bytes 393224 | tf_op jit(solution)/shard_map/ppermute | solution.py:273
  83.2 1.4 collective-permute-done.27.refs_4_
  84.6 2.0 %collective-permute-done.10.refs_1_.refs_5_ = bf16[512,128]{1,0:T(8,128)(2,1)S(1)} collective-permute-done((bf16[512,128]{1,0:T(8,128)(2,1)S(1)}, bf16[512,128]{1,0:T(8,128)(2,1)S(1)}, u32[]{:S(2)}, u32[]{:S(2)}) %collective-permute-start.10) | collective-permute-done | bytes 131104 | tf_op jit(solution)/shard_map/ppermute | solution.py:263
  86.6 1.4 collective-permute-done.22.refs_3_.refs_7_
  88.0 1.4 collective-permute-done.16.refs_2_.refs_6_
  89.4 1.4 collective-permute-done.4.refs_0_.refs_4_
  90.8 0.6 stage.12.refs_11_.refs_18_.refs_25_.refs_0_
  91.4 3.2 %collective-permute-start.28 = (bf16[512,128]{1,0:T(8,128)(2,1)S(1)}, bf16[512,128]{1,0:T(8,128)(2,1)S(1)}, u32[]{:S(2)}, u32[]{:S(2)}) collective-permute-start(bf16[512,128]{1,0:T(8,128)(2,1)S(1)} %stage.12.refs_11_.refs_18_.refs_25_.refs_0_), channel_id=1, source_target_pairs={{0,2},{2,4},{4,6},{1,7},{7,5},{5,3},{8,10},{10,12},{12,14},{9,15},... | collective-permute-start | bytes 393224 | tf_op jit(solution)/shard_map/ppermute | solution.py:273
  95.2 1.4 collective-permute-done.28.refs_4_
  96.5 2.0 %collective-permute-done.11.refs_1_.refs_5_ = bf16[512,128]{1,0:T(8,128)(2,1)S(1)} collective-permute-done((bf16[512,128]{1,0:T(8,128)(2,1)S(1)}, bf16[512,128]{1,0:T(8,128)(2,1)S(1)}, u32[]{:S(2)}, u32[]{:S(2)}) %collective-permute-start.11) | collective-permute-done | bytes 131104 | tf_op jit(solution)/shard_map/ppermute | solution.py:263
  98.5 1.4 collective-permute-done.23.refs_3_.refs_7_
  99.9 1.4 collective-permute-done.17.refs_2_.refs_6_
  101.3 1.4 collective-permute-done.5.refs_0_.refs_4_
  102.7 0.6 stage.13.refs_19_.refs_26_.refs_1_.refs_0_
  103.3 4.0 %collective-permute-start.33 = (bf16[512,128]{1,0:T(8,128)(2,1)S(1)}, bf16[512,128]{1,0:T(8,128)(2,1)S(1)}, u32[]{:S(2)}, u32[]{:S(2)}) collective-permute-start(bf16[512,128]{1,0:T(8,128)(2,1)S(1)} %stage.13.refs_19_.refs_26_.refs_1_.refs_0_), channel_id=1, source_target_pairs={{0,2},{2,4},{4,6},{1,7},{7,5},{5,3},{8,10},{10,12},{12,14},{9,15},... | collective-permute-start | bytes 393224 | tf_op jit(solution)/shard_map/ppermute | solution.py:273
  108.2 1.1 collective-permute-done.33.refs_4_
  109.3 2.1 %collective-permute-done.30.refs_1_.refs_13_ = bf16[512,128]{1,0:T(8,128)(2,1)S(1)} collective-permute-done((bf16[512,128]{1,0:T(8,128)(2,1)S(1)}, bf16[512,128]{1,0:T(8,128)(2,1)S(1)}, u32[]{:S(2)}, u32[]{:S(2)}) %collective-permute-start.30) | collective-permute-done | bytes 131104 | tf_op jit(solution)/shard_map/ppermute | solution.py:263
  111.4 1.3 collective-permute-done.32.refs_3_.refs_15_
  112.7 1.4 collective-permute-done.29.refs_0_.refs_12_
  114.1 1.4 collective-permute-done.31.refs_2_.refs_14_
  115.5 0.6 stage.14.refs_27_.refs_2_.refs_1_.refs_8_
  116.1 3.1 %collective-permute-start.38 = (bf16[512,128]{1,0:T(8,128)(2,1)S(1)}, bf16[512,128]{1,0:T(8,128)(2,1)S(1)}, u32[]{:S(2)}, u32[]{:S(2)}) collective-permute-start(bf16[512,128]{1,0:T(8,128)(2,1)S(1)} %stage.14.refs_27_.refs_2_.refs_1_.refs_8_), channel_id=1, source_target_pairs={{0,2},{2,4},{4,6},{1,7},{7,5},{5,3},{8,10},{10,12},{12,14},{9,15},... | collective-permute-start | bytes 393224 | tf_op jit(solution)/shard_map/ppermute | solution.py:273
  119.8 1.4 collective-permute-done.38.refs_4_
  121.1 2.2 %collective-permute-start.40 = (bf16[512,128]{1,0:T(8,128)(2,1)S(1)}, bf16[512,128]{1,0:T(8,128)(2,1)S(1)}, u32[]{:S(2)}, u32[]{:S(2)}) collective-permute-start(bf16[512,128]{1,0:T(8,128)(2,1)S(1)} %stage.14.refs_27_.refs_2_.refs_1_.refs_8_), channel_id=1, source_target_pairs={{0,6},{1,3},{8,14},{9,11},{16,22},{17,19},{24,30},{25,27},{34,32},... | collective-permute-start | bytes 393224 | tf_op jit(solution)/shard_map/ppermute | solution.py:273
  123.4 1.4 collective-permute-done.37.refs_3_.refs_23_
  124.8 1.1 collective-permute-done.34.refs_0_.refs_20_
  126.0 1.4 collective-permute-done.36.refs_2_.refs_22_
  128.0 3.2 %collective-permute-start.39 = (bf16[512,128]{1,0:T(8,128)(2,1)S(1)}, bf16[512,128]{1,0:T(8,128)(2,1)S(1)}, u32[]{:S(2)}, u32[]{:S(2)}) collective-permute-start(bf16[512,128]{1,0:T(8,128)(2,1)S(1)} %stage.15.refs_3_.refs_2_.refs_9_.refs_16_), channel_id=1, source_target_pairs={{0,2},{2,4},{4,6},{1,7},{7,5},{5,3},{8,10},{10,12},{12,14},{9,15},... | collective-permute-start | bytes 393224 | tf_op jit(solution)/shard_map/ppermute | solution.py:273
  131.2 2.7 %collective-permute-start.41 = (bf16[512,128]{1,0:T(8,128)(2,1)S(1)}, bf16[512,128]{1,0:T(8,128)(2,1)S(1)}, u32[]{:S(2)}, u32[]{:S(2)}) collective-permute-start(bf16[512,128]{1,0:T(8,128)(2,1)S(1)} %stage.15.refs_3_.refs_2_.refs_9_.refs_16_), channel_id=1, source_target_pairs={{0,4},{1,5},{8,12},{9,13},{16,20},{17,21},{24,28},{25,29},{34,38},... | collective-permute-start | bytes 393224 | tf_op jit(solution)/shard_map/ppermute | solution.py:273
  133.9 1.3 collective-permute-start.42
  135.2 2.1 %accumulate.3 = (f32[128,1024]{1,0:T(8,128)S(1)}, f32[128,1024]{1,0:T(8,128)S(1)}) custom-call(s32[5]{0:T(128)S(1)} %copy-done.3, bf16[512,128]{1,0:T(8,128)(2,1)S(1)} %stage.8.refs_0_, bf16[512,128]{1,0:T(8,128)(2,1)S(1)} %stage.9.refs_1_.refs_8_, bf16[512,128]{1,0:T(8,128)(2,1)S(1)} %stage.10.refs_2_.refs_9_.refs_16_, ...), custom_call_target="tpu_custom_call" | custom-call | flops 536870912 | tf_op jit(solution)/shard_map/accumulate/pallas_call | solution.py:212
  137.3 1.0 accumulate.4
  138.3 1.7 %accumulate.5 = (f32[128,1024]{1,0:T(8,128)S(1)}, f32[128,1024]{1,0:T(8,128)S(1)}) custom-call(s32[5]{0:T(128)S(1)} %copy-done.3, bf16[512,128]{1,0:T(8,128)(2,1)S(1)} %stage.13.refs_19_.refs_26_.refs_1_.refs_0_, bf16[512,128]{1,0:T(8,128)(2,1)S(1)} %stage.14.refs_27_.refs_2_.refs_1_.refs_8_, bf16[512,128]{1,0:T(8,128)(2,1)S(1)} %stage.15.refs_3_.refs_2_.refs_9_.refs_16_, ...), custom_call_target="tpu_custom_call" | custom-call | flops 402653184 | tf_op jit(solution)/shard_map/accumulate/pallas_call | solution.py:212
  140.1 11.5 %collective-permute-start.43 = (f32[128,1024]{1,0:T(8,128)S(1)}, f32[128,1024]{1,0:T(8,128)S(1)}, u32[]{:S(2)}, u32[]{:S(2)}) collective-permute-start(f32[128,1024]{1,0:T(8,128)S(1)} %get-tuple-element.20), channel_id=1, source_target_pairs={{0,1},{1,0},{2,3},{3,2},{4,5},{5,4},{6,7},{7,6},{8,9},{9,8},{10,11... | collective-permute-start | bytes 1572872 | tf_op jit(solution)/shard_map/ppermute | solution.py:300
  151.6 1.5 collective-permute-done.43
  153.1 0.9 add.9
  (48 shorter events, 6.0 us)
Async XLA Ops:
  7.5 28.0 %copy-start.2 = (bf16[512,128]{1,0:T(8,128)(2,1)S(1)}, bf16[512,128]{1,0:T(8,128)(2,1)}, u32[]{:S(2)}) copy-start(bf16[512,128]{1,0:T(8,128)(2,1)} %get-tuple-element.13.refs_0_.refs_4_) | copy-start | bytes 393220
  7.5 32.1 %copy-start.3 = (s32[5]{0:T(128)S(1)}, s32[5]{0:T(128)}, u32[]{:S(2)}) copy-start(s32[5]{0:T(128)} %stack.23.place_ref) | copy-start | bytes 64
  12.6 25.2 %collective-permute-start.18 = (bf16[512,128]{1,0:T(8,128)(2,1)}, bf16[512,128]{1,0:T(8,128)(2,1)S(1)}, u32[]{:S(2)}, u32[]{:S(2)}) collective-permute-start(bf16[512,128]{1,0:T(8,128)(2,1)} %transform_rest.1.refs_1_.refs_5_), channel_id=1, source_target_pairs={{0,8},{8,16},{16,24},{24,32},{32,40},{40,48},{48,56},{56,64},{64,7... | collective-permute-start | bytes 393224 | tf_op jit(solution)/shard_map/ppermute | solution.py:263
  35.5 4.1 %collective-permute-start.12 = (bf16[512,128]{1,0:T(8,128)(2,1)S(1)}, bf16[512,128]{1,0:T(8,128)(2,1)S(1)}, u32[]{:S(2)}, u32[]{:S(2)}) collective-permute-start(bf16[512,128]{1,0:T(8,128)(2,1)S(1)} %copy-done.2), channel_id=1, source_target_pairs={{0,8},{8,16},{16,24},{24,32},{32,40},{40,48},{48,56},{56,64},{64,7... | collective-permute-start | bytes 393224 | tf_op jit(solution)/shard_map/ppermute | solution.py:263
  35.6 10.5 %collective-permute-start.6 = (bf16[512,128]{1,0:T(8,128)(2,1)}, bf16[512,128]{1,0:T(8,128)(2,1)S(1)}, u32[]{:S(2)}, u32[]{:S(2)}) collective-permute-start(bf16[512,128]{1,0:T(8,128)(2,1)} %transform_rest.1.refs_1_.refs_5_), channel_id=1, source_target_pairs={{0,1},{1,0},{2,3},{3,2},{4,5},{5,4},{6,7},{7,6},{8,9},{9,8},{10,11... | collective-permute-start | bytes 393224 | tf_op jit(solution)/shard_map/ppermute | solution.py:256
  35.6 10.6 %collective-permute-start = (bf16[512,128]{1,0:T(8,128)(2,1)S(1)}, bf16[512,128]{1,0:T(8,128)(2,1)S(1)}, u32[]{:S(2)}, u32[]{:S(2)}) collective-permute-start(bf16[512,128]{1,0:T(8,128)(2,1)S(1)} %copy-done.2), channel_id=1, source_target_pairs={{0,1},{1,0},{2,3},{3,2},{4,5},{5,4},{6,7},{7,6},{8,9},{9,8},{10,11... | collective-permute-start | bytes 393224 | tf_op jit(solution)/shard_map/ppermute | solution.py:256
  39.7 0.9 copy-start
  41.2 6.7 %collective-permute-start.24 = (bf16[512,128]{1,0:T(8,128)(2,1)S(1)}, bf16[512,128]{1,0:T(8,128)(2,1)S(1)}, u32[]{:S(2)}, u32[]{:S(2)}) collective-permute-start(bf16[512,128]{1,0:T(8,128)(2,1)S(1)} %stage.8.refs_0_), channel_id=1, source_target_pairs={{0,2},{2,4},{4,6},{1,7},{7,5},{5,3},{8,10},{10,12},{12,14},{9,15},... | collective-permute-start | bytes 393224 | tf_op jit(solution)/shard_map/ppermute | solution.py:273
  46.0 3.9 %collective-permute-start.19 = (bf16[512,128]{1,0:T(8,128)(2,1)S(1)}, bf16[512,128]{1,0:T(8,128)(2,1)S(1)}, u32[]{:S(2)}, u32[]{:S(2)}) collective-permute-start(bf16[512,128]{1,0:T(8,128)(2,1)S(1)} %collective-permute-done.18.refs_3_.refs_7_), channel_id=1, source_target_pairs={{0,8},{8,16},{16,24},{24,32},{32,40},{40,48},{48,56},{56,64},{64,7... | collective-permute-start | bytes 393224 | tf_op jit(solution)/shard_map/ppermute | solution.py:263
  46.1 5.5 %collective-permute-start.7 = (bf16[512,128]{1,0:T(8,128)(2,1)S(1)}, bf16[512,128]{1,0:T(8,128)(2,1)S(1)}, u32[]{:S(2)}, u32[]{:S(2)}) collective-permute-start(bf16[512,128]{1,0:T(8,128)(2,1)S(1)} %collective-permute-done.6), channel_id=1, source_target_pairs={{0,8},{8,16},{16,24},{24,32},{32,40},{40,48},{48,56},{56,64},{64,7... | collective-permute-start | bytes 393224 | tf_op jit(solution)/shard_map/ppermute | solution.py:263
  46.3 6.7 %collective-permute-start.1 = (bf16[512,128]{1,0:T(8,128)(2,1)S(1)}, bf16[512,128]{1,0:T(8,128)(2,1)S(1)}, u32[]{:S(2)}, u32[]{:S(2)}) collective-permute-start(bf16[512,128]{1,0:T(8,128)(2,1)S(1)} %collective-permute-done), channel_id=1, source_target_pairs={{0,8},{8,16},{16,24},{24,32},{32,40},{40,48},{48,56},{56,64},{64,7... | collective-permute-start | bytes 393224 | tf_op jit(solution)/shard_map/ppermute | solution.py:263
  46.4 8.0 %collective-permute-start.13 = (bf16[512,128]{1,0:T(8,128)(2,1)S(1)}, bf16[512,128]{1,0:T(8,128)(2,1)S(1)}, u32[]{:S(2)}, u32[]{:S(2)}) collective-permute-start(bf16[512,128]{1,0:T(8,128)(2,1)S(1)} %collective-permute-done.12.refs_2_.refs_6_), channel_id=1, source_target_pairs={{0,8},{8,16},{16,24},{24,32},{32,40},{40,48},{48,56},{56,64},{64,7... | collective-permute-start | bytes 393224 | tf_op jit(solution)/shard_map/ppermute | solution.py:263
  55.0 5.4 %collective-permute-start.25 = (bf16[512,128]{1,0:T(8,128)(2,1)S(1)}, bf16[512,128]{1,0:T(8,128)(2,1)S(1)}, u32[]{:S(2)}, u32[]{:S(2)}) collective-permute-start(bf16[512,128]{1,0:T(8,128)(2,1)S(1)} %stage.9.refs_1_.refs_8_), channel_id=1, source_target_pairs={{0,2},{2,4},{4,6},{1,7},{7,5},{5,3},{8,10},{10,12},{12,14},{9,15},... | collective-permute-start | bytes 393224 | tf_op jit(solution)/shard_map/ppermute | solution.py:273
  58.5 3.9 %collective-permute-start.20 = (bf16[512,128]{1,0:T(8,128)(2,1)S(1)}, bf16[512,128]{1,0:T(8,128)(2,1)S(1)}, u32[]{:S(2)}, u32[]{:S(2)}) collective-permute-start(bf16[512,128]{1,0:T(8,128)(2,1)S(1)} %collective-permute-done.19.refs_3_.refs_15_), channel_id=1, source_target_pairs={{0,8},{8,16},{16,24},{24,32},{32,40},{40,48},{48,56},{56,64},{64,7... | collective-permute-start | bytes 393224 | tf_op jit(solution)/shard_map/ppermute | solution.py:263
  58.6 5.2 %collective-permute-start.8 = (bf16[512,128]{1,0:T(8,128)(2,1)S(1)}, bf16[512,128]{1,0:T(8,128)(2,1)S(1)}, u32[]{:S(2)}, u32[]{:S(2)}) collective-permute-start(bf16[512,128]{1,0:T(8,128)(2,1)S(1)} %collective-permute-done.7.refs_1_.refs_13_), channel_id=1, source_target_pairs={{0,8},{8,16},{16,24},{24,32},{32,40},{40,48},{48,56},{56,64},{64,7... | collective-permute-start | bytes 393224 | tf_op jit(solution)/shard_map/ppermute | solution.py:263
  58.8 6.8 %collective-permute-start.14 = (bf16[512,128]{1,0:T(8,128)(2,1)S(1)}, bf16[512,128]{1,0:T(8,128)(2,1)S(1)}, u32[]{:S(2)}, u32[]{:S(2)}) collective-permute-start(bf16[512,128]{1,0:T(8,128)(2,1)S(1)} %collective-permute-done.13.refs_2_.refs_14_), channel_id=1, source_target_pairs={{0,8},{8,16},{16,24},{24,32},{32,40},{40,48},{48,56},{56,64},{64,7... | collective-permute-start | bytes 393224 | tf_op jit(solution)/shard_map/ppermute | solution.py:263
  58.9 8.0 %collective-permute-start.2 = (bf16[512,128]{1,0:T(8,128)(2,1)S(1)}, bf16[512,128]{1,0:T(8,128)(2,1)S(1)}, u32[]{:S(2)}, u32[]{:S(2)}) collective-permute-start(bf16[512,128]{1,0:T(8,128)(2,1)S(1)} %collective-permute-done.1.refs_0_.refs_12_), channel_id=1, source_target_pairs={{0,8},{8,16},{16,24},{24,32},{32,40},{40,48},{48,56},{56,64},{64,7... | collective-permute-start | bytes 393224 | tf_op jit(solution)/shard_map/ppermute | solution.py:263
  67.5 4.9 %collective-permute-start.26 = (bf16[512,128]{1,0:T(8,128)(2,1)S(1)}, bf16[512,128]{1,0:T(8,128)(2,1)S(1)}, u32[]{:S(2)}, u32[]{:S(2)}) collective-permute-start(bf16[512,128]{1,0:T(8,128)(2,1)S(1)} %stage.10.refs_2_.refs_9_.refs_16_), channel_id=1, source_target_pairs={{0,2},{2,4},{4,6},{1,7},{7,5},{5,3},{8,10},{10,12},{12,14},{9,15},... | collective-permute-start | bytes 393224 | tf_op jit(solution)/shard_map/ppermute | solution.py:273
  70.5 4.1 %collective-permute-start.21 = (bf16[512,128]{1,0:T(8,128)(2,1)S(1)}, bf16[512,128]{1,0:T(8,128)(2,1)S(1)}, u32[]{:S(2)}, u32[]{:S(2)}) collective-permute-start(bf16[512,128]{1,0:T(8,128)(2,1)S(1)} %collective-permute-done.20.refs_3_.refs_23_), channel_id=1, source_target_pairs={{0,8},{8,16},{16,24},{24,32},{32,40},{40,48},{48,56},{56,64},{64,7... | collective-permute-start | bytes 393224 | tf_op jit(solution)/shard_map/ppermute | solution.py:263
  70.8 5.2 %collective-permute-start.9 = (bf16[512,128]{1,0:T(8,128)(2,1)S(1)}, bf16[512,128]{1,0:T(8,128)(2,1)S(1)}, u32[]{:S(2)}, u32[]{:S(2)}) collective-permute-start(bf16[512,128]{1,0:T(8,128)(2,1)S(1)} %collective-permute-done.8.refs_1_.refs_21_), channel_id=1, source_target_pairs={{0,8},{8,16},{16,24},{24,32},{32,40},{40,48},{48,56},{56,64},{64,7... | collective-permute-start | bytes 393224 | tf_op jit(solution)/shard_map/ppermute | solution.py:263
  70.9 6.5 %collective-permute-start.15 = (bf16[512,128]{1,0:T(8,128)(2,1)S(1)}, bf16[512,128]{1,0:T(8,128)(2,1)S(1)}, u32[]{:S(2)}, u32[]{:S(2)}) collective-permute-start(bf16[512,128]{1,0:T(8,128)(2,1)S(1)} %collective-permute-done.14.refs_2_.refs_22_), channel_id=1, source_target_pairs={{0,8},{8,16},{16,24},{24,32},{32,40},{40,48},{48,56},{56,64},{64,7... | collective-permute-start | bytes 393224 | tf_op jit(solution)/shard_map/ppermute | solution.py:263
  71.1 7.7 %collective-permute-start.3 = (bf16[512,128]{1,0:T(8,128)(2,1)S(1)}, bf16[512,128]{1,0:T(8,128)(2,1)S(1)}, u32[]{:S(2)}, u32[]{:S(2)}) collective-permute-start(bf16[512,128]{1,0:T(8,128)(2,1)S(1)} %collective-permute-done.2.refs_0_.refs_20_), channel_id=1, source_target_pairs={{0,8},{8,16},{16,24},{24,32},{32,40},{40,48},{48,56},{56,64},{64,7... | collective-permute-start | bytes 393224 | tf_op jit(solution)/shard_map/ppermute | solution.py:263
  79.4 5.2 %collective-permute-start.27 = (bf16[512,128]{1,0:T(8,128)(2,1)S(1)}, bf16[512,128]{1,0:T(8,128)(2,1)S(1)}, u32[]{:S(2)}, u32[]{:S(2)}) collective-permute-start(bf16[512,128]{1,0:T(8,128)(2,1)S(1)} %stage.11.refs_3_.refs_10_.refs_17_.refs_24_), channel_id=1, source_target_pairs={{0,2},{2,4},{4,6},{1,7},{7,5},{5,3},{8,10},{10,12},{12,14},{9,15},... | collective-permute-start | bytes 393224 | tf_op jit(solution)/shard_map/ppermute | solution.py:273
  82.6 3.9 %collective-permute-start.10 = (bf16[512,128]{1,0:T(8,128)(2,1)S(1)}, bf16[512,128]{1,0:T(8,128)(2,1)S(1)}, u32[]{:S(2)}, u32[]{:S(2)}) collective-permute-start(bf16[512,128]{1,0:T(8,128)(2,1)S(1)} %collective-permute-done.9.refs_1_.refs_29_), channel_id=1, source_target_pairs={{0,8},{8,16},{16,24},{24,32},{32,40},{40,48},{48,56},{56,64},{64,7... | collective-permute-start | bytes 393224 | tf_op jit(solution)/shard_map/ppermute | solution.py:263
  82.8 5.2 %collective-permute-start.22 = (bf16[512,128]{1,0:T(8,128)(2,1)S(1)}, bf16[512,128]{1,0:T(8,128)(2,1)S(1)}, u32[]{:S(2)}, u32[]{:S(2)}) collective-permute-start(bf16[512,128]{1,0:T(8,128)(2,1)S(1)} %collective-permute-done.21.refs_3_.refs_31_), channel_id=1, source_target_pairs={{0,8},{8,16},{16,24},{24,32},{32,40},{40,48},{48,56},{56,64},{64,7... | collective-permute-start | bytes 393224 | tf_op jit(solution)/shard_map/ppermute | solution.py:263
  82.9 6.5 %collective-permute-start.16 = (bf16[512,128]{1,0:T(8,128)(2,1)S(1)}, bf16[512,128]{1,0:T(8,128)(2,1)S(1)}, u32[]{:S(2)}, u32[]{:S(2)}) collective-permute-start(bf16[512,128]{1,0:T(8,128)(2,1)S(1)} %collective-permute-done.15.refs_2_.refs_30_), channel_id=1, source_target_pairs={{0,8},{8,16},{16,24},{24,32},{32,40},{40,48},{48,56},{56,64},{64,7... | collective-permute-start | bytes 393224 | tf_op jit(solution)/shard_map/ppermute | solution.py:263
  83.1 7.7 %collective-permute-start.4 = (bf16[512,128]{1,0:T(8,128)(2,1)S(1)}, bf16[512,128]{1,0:T(8,128)(2,1)S(1)}, u32[]{:S(2)}, u32[]{:S(2)}) collective-permute-start(bf16[512,128]{1,0:T(8,128)(2,1)S(1)} %collective-permute-done.3.refs_0_.refs_28_), channel_id=1, source_target_pairs={{0,8},{8,16},{16,24},{24,32},{32,40},{40,48},{48,56},{56,64},{64,7... | collective-permute-start | bytes 393224 | tf_op jit(solution)/shard_map/ppermute | solution.py:263
  91.4 5.1 %collective-permute-start.28 = (bf16[512,128]{1,0:T(8,128)(2,1)S(1)}, bf16[512,128]{1,0:T(8,128)(2,1)S(1)}, u32[]{:S(2)}, u32[]{:S(2)}) collective-permute-start(bf16[512,128]{1,0:T(8,128)(2,1)S(1)} %stage.12.refs_11_.refs_18_.refs_25_.refs_0_), channel_id=1, source_target_pairs={{0,2},{2,4},{4,6},{1,7},{7,5},{5,3},{8,10},{10,12},{12,14},{9,15},... | collective-permute-start | bytes 393224 | tf_op jit(solution)/shard_map/ppermute | solution.py:273
  94.6 3.9 %collective-permute-start.11 = (bf16[512,128]{1,0:T(8,128)(2,1)S(1)}, bf16[512,128]{1,0:T(8,128)(2,1)S(1)}, u32[]{:S(2)}, u32[]{:S(2)}) collective-permute-start(bf16[512,128]{1,0:T(8,128)(2,1)S(1)} %collective-permute-done.10.refs_1_.refs_5_), channel_id=1, source_target_pairs={{0,8},{8,16},{16,24},{24,32},{32,40},{40,48},{48,56},{56,64},{64,7... | collective-permute-start | bytes 393224 | tf_op jit(solution)/shard_map/ppermute | solution.py:263
  94.7 5.2 %collective-permute-start.23 = (bf16[512,128]{1,0:T(8,128)(2,1)S(1)}, bf16[512,128]{1,0:T(8,128)(2,1)S(1)}, u32[]{:S(2)}, u32[]{:S(2)}) collective-permute-start(bf16[512,128]{1,0:T(8,128)(2,1)S(1)} %collective-permute-done.22.refs_3_.refs_7_), channel_id=1, source_target_pairs={{0,8},{8,16},{16,24},{24,32},{32,40},{40,48},{48,56},{56,64},{64,7... | collective-permute-start | bytes 393224 | tf_op jit(solution)/shard_map/ppermute | solution.py:263
  94.9 6.5 %collective-permute-start.17 = (bf16[512,128]{1,0:T(8,128)(2,1)S(1)}, bf16[512,128]{1,0:T(8,128)(2,1)S(1)}, u32[]{:S(2)}, u32[]{:S(2)}) collective-permute-start(bf16[512,128]{1,0:T(8,128)(2,1)S(1)} %collective-permute-done.16.refs_2_.refs_6_), channel_id=1, source_target_pairs={{0,8},{8,16},{16,24},{24,32},{32,40},{40,48},{48,56},{56,64},{64,7... | collective-permute-start | bytes 393224 | tf_op jit(solution)/shard_map/ppermute | solution.py:263
  95.0 7.7 %collective-permute-start.5 = (bf16[512,128]{1,0:T(8,128)(2,1)S(1)}, bf16[512,128]{1,0:T(8,128)(2,1)S(1)}, u32[]{:S(2)}, u32[]{:S(2)}) collective-permute-start(bf16[512,128]{1,0:T(8,128)(2,1)S(1)} %collective-permute-done.4.refs_0_.refs_4_), channel_id=1, source_target_pairs={{0,8},{8,16},{16,24},{24,32},{32,40},{40,48},{48,56},{56,64},{64,7... | collective-permute-start | bytes 393224 | tf_op jit(solution)/shard_map/ppermute | solution.py:263
  103.3 6.0 %collective-permute-start.33 = (bf16[512,128]{1,0:T(8,128)(2,1)S(1)}, bf16[512,128]{1,0:T(8,128)(2,1)S(1)}, u32[]{:S(2)}, u32[]{:S(2)}) collective-permute-start(bf16[512,128]{1,0:T(8,128)(2,1)S(1)} %stage.13.refs_19_.refs_26_.refs_1_.refs_0_), channel_id=1, source_target_pairs={{0,2},{2,4},{4,6},{1,7},{7,5},{5,3},{8,10},{10,12},{12,14},{9,15},... | collective-permute-start | bytes 393224 | tf_op jit(solution)/shard_map/ppermute | solution.py:273
  107.4 4.0 %collective-permute-start.30 = (bf16[512,128]{1,0:T(8,128)(2,1)S(1)}, bf16[512,128]{1,0:T(8,128)(2,1)S(1)}, u32[]{:S(2)}, u32[]{:S(2)}) collective-permute-start(bf16[512,128]{1,0:T(8,128)(2,1)S(1)} %collective-permute-done.11.refs_1_.refs_5_), channel_id=1, source_target_pairs={{0,8},{8,16},{16,24},{24,32},{32,40},{40,48},{48,56},{56,64},{64,7... | collective-permute-start | bytes 393224 | tf_op jit(solution)/shard_map/ppermute | solution.py:263
  107.5 5.2 %collective-permute-start.32 = (bf16[512,128]{1,0:T(8,128)(2,1)S(1)}, bf16[512,128]{1,0:T(8,128)(2,1)S(1)}, u32[]{:S(2)}, u32[]{:S(2)}) collective-permute-start(bf16[512,128]{1,0:T(8,128)(2,1)S(1)} %collective-permute-done.23.refs_3_.refs_7_), channel_id=1, source_target_pairs={{0,8},{8,16},{16,24},{24,32},{32,40},{40,48},{48,56},{56,64},{64,7... | collective-permute-start | bytes 393224 | tf_op jit(solution)/shard_map/ppermute | solution.py:263
  107.7 6.5 %collective-permute-start.29 = (bf16[512,128]{1,0:T(8,128)(2,1)S(1)}, bf16[512,128]{1,0:T(8,128)(2,1)S(1)}, u32[]{:S(2)}, u32[]{:S(2)}) collective-permute-start(bf16[512,128]{1,0:T(8,128)(2,1)S(1)} %collective-permute-done.5.refs_0_.refs_4_), channel_id=1, source_target_pairs={{0,8},{8,16},{16,24},{24,32},{32,40},{40,48},{48,56},{56,64},{64,7... | collective-permute-start | bytes 393224 | tf_op jit(solution)/shard_map/ppermute | solution.py:263
  107.8 7.7 %collective-permute-start.31 = (bf16[512,128]{1,0:T(8,128)(2,1)S(1)}, bf16[512,128]{1,0:T(8,128)(2,1)S(1)}, u32[]{:S(2)}, u32[]{:S(2)}) collective-permute-start(bf16[512,128]{1,0:T(8,128)(2,1)S(1)} %collective-permute-done.17.refs_2_.refs_6_), channel_id=1, source_target_pairs={{0,8},{8,16},{16,24},{24,32},{32,40},{40,48},{48,56},{56,64},{64,7... | collective-permute-start | bytes 393224 | tf_op jit(solution)/shard_map/ppermute | solution.py:263
  116.1 19.1 %copy-start.1 = (bf16[512,128]{1,0:T(8,128)(2,1)S(1)}, bf16[512,128]{1,0:T(8,128)(2,1)}, u32[]{:S(2)}) copy-start(bf16[512,128]{1,0:T(8,128)(2,1)} %transform_rest.1.refs_1_.refs_5_) | copy-start | bytes 393220
  116.1 5.0 %collective-permute-start.38 = (bf16[512,128]{1,0:T(8,128)(2,1)S(1)}, bf16[512,128]{1,0:T(8,128)(2,1)S(1)}, u32[]{:S(2)}, u32[]{:S(2)}) collective-permute-start(bf16[512,128]{1,0:T(8,128)(2,1)S(1)} %stage.14.refs_27_.refs_2_.refs_1_.refs_8_), channel_id=1, source_target_pairs={{0,2},{2,4},{4,6},{1,7},{7,5},{5,3},{8,10},{10,12},{12,14},{9,15},... | collective-permute-start | bytes 393224 | tf_op jit(solution)/shard_map/ppermute | solution.py:273
  119.2 4.2 %collective-permute-start.35 = (bf16[512,128]{1,0:T(8,128)(2,1)S(1)}, bf16[512,128]{1,0:T(8,128)(2,1)S(1)}, u32[]{:S(2)}, u32[]{:S(2)}) collective-permute-start(bf16[512,128]{1,0:T(8,128)(2,1)S(1)} %collective-permute-done.30.refs_1_.refs_13_), channel_id=1, source_target_pairs={{0,8},{8,16},{16,24},{24,32},{32,40},{40,48},{48,56},{56,64},{64,7... | collective-permute-start | bytes 393224 | tf_op jit(solution)/shard_map/ppermute | solution.py:263
  119.4 5.5 %collective-permute-start.37 = (bf16[512,128]{1,0:T(8,128)(2,1)S(1)}, bf16[512,128]{1,0:T(8,128)(2,1)S(1)}, u32[]{:S(2)}, u32[]{:S(2)}) collective-permute-start(bf16[512,128]{1,0:T(8,128)(2,1)S(1)} %collective-permute-done.32.refs_3_.refs_15_), channel_id=1, source_target_pairs={{0,8},{8,16},{16,24},{24,32},{32,40},{40,48},{48,56},{56,64},{64,7... | collective-permute-start | bytes 393224 | tf_op jit(solution)/shard_map/ppermute | solution.py:263
  119.5 6.5 %collective-permute-start.34 = (bf16[512,128]{1,0:T(8,128)(2,1)S(1)}, bf16[512,128]{1,0:T(8,128)(2,1)S(1)}, u32[]{:S(2)}, u32[]{:S(2)}) collective-permute-start(bf16[512,128]{1,0:T(8,128)(2,1)S(1)} %collective-permute-done.29.refs_0_.refs_12_), channel_id=1, source_target_pairs={{0,8},{8,16},{16,24},{24,32},{32,40},{40,48},{48,56},{56,64},{64,7... | collective-permute-start | bytes 393224 | tf_op jit(solution)/shard_map/ppermute | solution.py:263
  119.6 7.7 %collective-permute-start.36 = (bf16[512,128]{1,0:T(8,128)(2,1)S(1)}, bf16[512,128]{1,0:T(8,128)(2,1)S(1)}, u32[]{:S(2)}, u32[]{:S(2)}) collective-permute-start(bf16[512,128]{1,0:T(8,128)(2,1)S(1)} %collective-permute-done.31.refs_2_.refs_14_), channel_id=1, source_target_pairs={{0,8},{8,16},{16,24},{24,32},{32,40},{40,48},{48,56},{56,64},{64,7... | collective-permute-start | bytes 393224 | tf_op jit(solution)/shard_map/ppermute | solution.py:263
  121.1 17.2 %collective-permute-start.40 = (bf16[512,128]{1,0:T(8,128)(2,1)S(1)}, bf16[512,128]{1,0:T(8,128)(2,1)S(1)}, u32[]{:S(2)}, u32[]{:S(2)}) collective-permute-start(bf16[512,128]{1,0:T(8,128)(2,1)S(1)} %stage.14.refs_27_.refs_2_.refs_1_.refs_8_), channel_id=1, source_target_pairs={{0,6},{1,3},{8,14},{9,11},{16,22},{17,19},{24,30},{25,27},{34,32},... | collective-permute-start | bytes 393224 | tf_op jit(solution)/shard_map/ppermute | solution.py:273
  128.0 10.4 %collective-permute-start.39 = (bf16[512,128]{1,0:T(8,128)(2,1)S(1)}, bf16[512,128]{1,0:T(8,128)(2,1)S(1)}, u32[]{:S(2)}, u32[]{:S(2)}) collective-permute-start(bf16[512,128]{1,0:T(8,128)(2,1)S(1)} %stage.15.refs_3_.refs_2_.refs_9_.refs_16_), channel_id=1, source_target_pairs={{0,2},{2,4},{4,6},{1,7},{7,5},{5,3},{8,10},{10,12},{12,14},{9,15},... | collective-permute-start | bytes 393224 | tf_op jit(solution)/shard_map/ppermute | solution.py:273
  131.2 7.1 %collective-permute-start.41 = (bf16[512,128]{1,0:T(8,128)(2,1)S(1)}, bf16[512,128]{1,0:T(8,128)(2,1)S(1)}, u32[]{:S(2)}, u32[]{:S(2)}) collective-permute-start(bf16[512,128]{1,0:T(8,128)(2,1)S(1)} %stage.15.refs_3_.refs_2_.refs_9_.refs_16_), channel_id=1, source_target_pairs={{0,4},{1,5},{8,12},{9,13},{16,20},{17,21},{24,28},{25,29},{34,38},... | collective-permute-start | bytes 393224 | tf_op jit(solution)/shard_map/ppermute | solution.py:273
  133.9 4.5 %collective-permute-start.42 = (bf16[512,128]{1,0:T(8,128)(2,1)S(1)}, bf16[512,128]{1,0:T(8,128)(2,1)S(1)}, u32[]{:S(2)}, u32[]{:S(2)}) collective-permute-start(bf16[512,128]{1,0:T(8,128)(2,1)S(1)} %stage.15.refs_3_.refs_2_.refs_9_.refs_16_), channel_id=1, source_target_pairs={{0,6},{1,3},{8,14},{9,11},{16,22},{17,19},{24,30},{25,27},{34,32},... | collective-permute-start | bytes 393224 | tf_op jit(solution)/shard_map/ppermute | solution.py:273
  140.1 13.1 %collective-permute-start.43 = (f32[128,1024]{1,0:T(8,128)S(1)}, f32[128,1024]{1,0:T(8,128)S(1)}, u32[]{:S(2)}, u32[]{:S(2)}) collective-permute-start(f32[128,1024]{1,0:T(8,128)S(1)} %get-tuple-element.20), channel_id=1, source_target_pairs={{0,1},{1,0},{2,3},{3,2},{4,5},{5,4},{6,7},{7,6},{8,9},{9,8},{10,11... | collective-permute-start | bytes 1572872 | tf_op jit(solution)/shard_map/ppermute | solution.py:300

commit v2 on v1

v2 whole, which is shorter than its diff:
```python
import functools

import jax
import jax.numpy as jnp
from jax import lax
from jax.experimental import pallas as pl
from jax.experimental.pallas import tpu as pltpu
from jax.sharding import PartitionSpec as P


VMEM_BYTES = 12 * 1024 * 1024
TRANSFORM_VMEM_BYTES = 60 * 1024 * 1024
BATCH_ENDS = (3, 6)


def contract_last(left, right):
    return lax.dot_general(
        left, right, (((1,), (1,)), ((), ())), preferred_element_type=jnp.float32
    )


def transform_kernel(
    build, n_basis, block0, index_ref, nu_ref, mask_ref, assign_ref, metric_ref,
    table_or_orbitals_ref, tiles_ref, out_ref, *rest
):
    n_p, row_blocks, slots, tile, _ = tiles_ref.shape
    lanes = out_ref.shape[1]
    n_i = lanes // n_p
    step = pl.program_id(0)
    if build:
        table_ref, lane_mask_ref, held_ref, tile_sem, rows_ref, row_sem = rest
    else:
        table_ref = table_or_orbitals_ref
        lane_mask_ref, held_ref, tile_sem = rest
    blocks = table_ref.shape[0] // tile - 1
    n_blocks = held_ref.shape[0]

    def fetch(m, p):
        return pltpu.make_async_copy(
            tiles_ref.at[p, block0 + m], held_ref.at[m, p], tile_sem.at[m, p]
        )

    @pl.when(step == 0)
    def _():
        if build:
            group = rows_ref.shape[1]

            def row_copy(i):
                at = pl.ds(pl.multiple_of(index_ref[i] // group * group, group), group)
                return pltpu.make_async_copy(
                    table_or_orbitals_ref.at[at, :], rows_ref.at[i], row_sem.at[i]
                )

            for i in range(n_i):
                row_copy(i).start()
        for m in range(n_blocks):
            for p in range(n_p):
                fetch(m, p).start()
        lane = lax.broadcasted_iota(jnp.int32, (16, lanes), 1)
        for p in range(n_p):
            lane_mask_ref[p] = jnp.where(lane // n_i == p, 1.0, 0.0).astype(jnp.bfloat16)
        if build:
            row = lax.broadcasted_iota(jnp.int32, (n_i * group, lanes), 0)
            col = lax.broadcasted_iota(jnp.int32, (n_i * group, lanes), 1)
            wanted = jnp.zeros((n_i * group, lanes), jnp.int32)
            for i in range(n_i):
                wanted = jnp.where(col % n_i == i, i * group + index_ref[i] % group, wanted)
            one_hot = jnp.where(row == wanted, 1.0, 0.0).astype(jnp.bfloat16)
            table_ref[pl.ds((blocks - 1) * tile, 2 * tile), :] = jnp.zeros(
                (2 * tile, lanes), jnp.bfloat16
            )
            for i in range(n_i):
                row_copy(i).wait()
            for k in range(blocks):
                wide = min(tile, n_basis - k * tile)
                got = rows_ref[:, :, k * tile : k * tile + wide].reshape(n_i * group, wide)
                turned = lax.dot_general(
                    got, one_hot, (((0,), (0,)), ((), ())), preferred_element_type=jnp.float32
                )
                table_ref[k * tile : k * tile + wide, :] = turned.astype(jnp.bfloat16)

    for p in range(n_p):
        fetch(step, p).wait()
    total = jnp.zeros((tile, lanes), jnp.float32)
    for p in range(n_p):
        lane_mask = lane_mask_ref[p]
        for s in range(0, slots, 2):
            weights = []
            for t in (s, s + 1):
                nu = jnp.where(mask_ref[p, t, block0 + step] > 0, nu_ref[p, t, block0 + step], blocks)
                part = table_ref[pl.ds(pl.multiple_of(nu * tile, tile), tile), :]
                part = part.reshape(tile // 16, 16, lanes) * lane_mask[None]
                weights.append(part.reshape(tile, lanes))
            left = jnp.concatenate([held_ref[step, p, s], held_ref[step, p, s + 1]], axis=1)
            total = total + jnp.dot(
                left, jnp.concatenate(weights, axis=0), preferred_element_type=jnp.float32
            )
    lane = lax.broadcasted_iota(jnp.int32, (1, lanes), 1)
    factors = jnp.zeros((1, lanes), jnp.float32)
    for p in range(n_p):
        factors = jnp.where(lane // n_i == p, metric_ref[assign_ref[p]], factors)
    first = (lax.axis_index("orb") * row_blocks + block0 + step) * tile
    row = first + lax.broadcasted_iota(jnp.int32, (tile, lanes), 0)
    out_ref[...] = jnp.where(row < n_basis, total * factors, 0.0).astype(out_ref.dtype)


def transform(build, block0, n_blocks, n_basis, scalars, table, b_tiles):
    n_p, _, slots, tile, _ = b_tiles.shape
    n_i = scalars[0].shape[0]
    lanes = n_p * n_i
    blocks = (n_basis + tile - 1) // tile
    smem = pl.BlockSpec(memory_space=pltpu.SMEM)
    vmem = pl.BlockSpec(memory_space=pltpu.VMEM)
    hbm = pl.BlockSpec(memory_space=pl.ANY)
    out_shape = [jax.ShapeDtypeStruct((n_blocks * tile, lanes), jnp.bfloat16)]
    out_specs = [pl.BlockSpec((tile, lanes), lambda m: (m, 0))]
    scratch = [
        pltpu.VMEM((n_p, 16, lanes), jnp.bfloat16),
        pltpu.VMEM((n_blocks, n_p, slots, tile, tile), b_tiles.dtype),
        pltpu.SemaphoreType.DMA((n_blocks, n_p)),
    ]
    if build:
        out_shape.append(jax.ShapeDtypeStruct(((blocks + 1) * tile, lanes), jnp.bfloat16))
        out_specs.append(vmem)
        scratch += [
            pltpu.VMEM((n_i, 8, n_basis), jnp.bfloat16),
            pltpu.SemaphoreType.DMA((n_i,)),
        ]
    return pl.pallas_call(
        functools.partial(transform_kernel, build, n_basis, block0),
        grid=(n_blocks,),
        out_shape=out_shape,
        in_specs=[smem] * len(scalars) + [hbm if build else vmem, hbm],
        out_specs=out_specs,
        scratch_shapes=scratch,
        compiler_params=pltpu.CompilerParams(vmem_limit_bytes=TRANSFORM_VMEM_BYTES),
        cost_estimate=pl.CostEstimate(
            flops=2 * n_blocks * n_p * slots * tile * tile * lanes,
            bytes_accessed=2 * n_blocks * n_p * slots * tile * tile,
            transcendentals=0,
        ),
        name="transform_first" if build else "transform_rest",
    )(*scalars, table, b_tiles)


def place_of(plane_rows, mu_dev):
    per_orb = mu_dev // plane_rows
    z, x, core = lax.axis_index("aux"), lax.axis_index("orb"), lax.axis_index("occ")
    n_orb = lax.axis_size("orb")
    away = x - z // per_orb
    link = lax.rem(jnp.where(core == 0, away, -away) + n_orb, n_orb)
    return link, core, lax.rem(z, per_orb) * plane_rows


def stage_kernel(plane_rows, counts, *refs):
    *parts, out_ref = refs
    mu_dev = sum(p.shape[0] for p in parts[: counts[0]])
    _, _, first = place_of(plane_rows, mu_dev)
    used = 0
    for k, count in enumerate(counts):
        start = 0
        for part in parts[used : used + count]:
            size = part.shape[0]

            @pl.when((first >= start) & (first < start + size))
            def _():
                at = pl.ds(pl.multiple_of(first - start, plane_rows), plane_rows)
                out_ref[k * plane_rows : (k + 1) * plane_rows, :] = part[at, :]

            start += size
        used += count


def stage(slabs, plane_rows):
    vmem = pl.BlockSpec(memory_space=pltpu.VMEM)
    parts = [p for s in slabs for p in s]
    return pl.pallas_call(
        functools.partial(stage_kernel, plane_rows, tuple(len(s) for s in slabs)),
        out_shape=jax.ShapeDtypeStruct((len(slabs) * plane_rows, parts[0].shape[1]), parts[0].dtype),
        in_specs=[vmem] * len(parts),
        out_specs=vmem,
        compiler_params=pltpu.CompilerParams(vmem_limit_bytes=VMEM_BYTES),
        cost_estimate=pl.CostEstimate(flops=1000000, bytes_accessed=0, transcendentals=0),
        name="stage",
    )(*parts)


def choose_kernel(plane_rows, mu_dev, own_ref, came_ref, out_ref):
    link, _, _ = place_of(plane_rows, mu_dev)

    @pl.when(link == 0)
    def _():
        out_ref[...] = own_ref[...]

    @pl.when(link != 0)
    def _():
        out_ref[...] = came_ref[...]


def choose(own, came, plane_rows, mu_dev):
    vmem = pl.BlockSpec(memory_space=pltpu.VMEM)
    return pl.pallas_call(
        functools.partial(choose_kernel, plane_rows, mu_dev),
        out_shape=jax.ShapeDtypeStruct(own.shape, own.dtype),
        in_specs=[vmem] * 2,
        out_specs=vmem,
        compiler_params=pltpu.CompilerParams(vmem_limit_bytes=VMEM_BYTES),
        cost_estimate=pl.CostEstimate(flops=1000000, bytes_accessed=0, transcendentals=0),
        name="choose",
    )(own, came)


def accumulate_kernel(n_candidates, counts, has_prev, *refs):
    candidates = refs[:n_candidates]
    parts = refs[n_candidates : n_candidates + sum(counts)]
    rest = refs[n_candidates + sum(counts) :]
    prev, outs = (rest[:2], rest[2:]) if has_prev else (None, rest)
    slabs, used = [], 0
    for count in counts:
        slabs.append(parts[used : used + count])
        used += count
    n = len(slabs)
    mine, mu_dev = outs[0].shape
    plane_rows = candidates[0].shape[0] // n
    link, core, _ = place_of(plane_rows, mu_dev)
    groups = [range(j, min(j + 2, n)) for j in range(0, n, 2)]

    def rows_at(j, side):
        which = core if side == 0 else 1 - core
        at = pl.ds(pl.multiple_of(j * plane_rows + which * mine, mine), mine)
        c = [r[at, :] for r in candidates]
        if n_candidates == 2:
            return jnp.where(link < 2, c[0], c[1])
        return jnp.where(link < 2, jnp.where(link == 0, c[0], c[1]), jnp.where(link == 2, c[2], c[3]))

    left = [
        [jnp.concatenate([rows_at(j, side) for j in g], axis=1) for side in range(2)] for g in groups
    ]
    step = 256

    def cut(slab, start):
        for part in slab:
            if start < part.shape[0]:
                return part[start : start + step, :]
            start -= part.shape[0]

    for start in range(0, mu_dev, step):
        right = [jnp.concatenate([cut(slabs[j], start) for j in g], axis=1) for g in groups]
        for side in range(2):
            acc = prev[side][:, start : start + step] if has_prev else None
            for k in range(len(groups)):
                part = contract_last(left[k][side], right[k])
                acc = part if acc is None else acc + part
            outs[side][:, start : start + step] = acc


def accumulate(candidates, slabs, prev, block_rows, mu_dev):
    counts = tuple(len(s) for s in slabs)
    has_prev = prev is not None
    operands = list(candidates) + [p for s in slabs for p in s] + (list(prev) if has_prev else [])
    vmem = pl.BlockSpec(memory_space=pltpu.VMEM)
    flops = 2 * 2 * block_rows * mu_dev * len(slabs) * slabs[0][0].shape[1]
    return pl.pallas_call(
        functools.partial(accumulate_kernel, len(candidates), counts, has_prev),
        out_shape=[jax.ShapeDtypeStruct((block_rows, mu_dev), jnp.float32)] * 2,
        in_specs=[vmem] * len(operands),
        out_specs=[vmem] * 2,
        compiler_params=pltpu.CompilerParams(vmem_limit_bytes=VMEM_BYTES),
        cost_estimate=pl.CostEstimate(flops=flops, bytes_accessed=0, transcendentals=0),
        name="accumulate",
    )(*operands)


def per_device(b_tiles, nu_block, tile_mask, assignment, metric_factor, orbitals, occupied_index):
    row_blocks, tile_size = b_tiles.shape[1], b_tiles.shape[3]
    n_basis = orbitals.shape[1]
    padded = (n_basis + tile_size - 1) // tile_size * tile_size
    mu_dev = row_blocks * tile_size
    n_aux, n_orb, n_occ = lax.axis_size("aux"), lax.axis_size("orb"), lax.axis_size("occ")
    block_rows = padded // (n_aux * n_occ)
    plane_rows = block_rows * n_occ
    per_orb = mu_dev // plane_rows

    scalars = (
        occupied_index,
        nu_block.transpose(0, 2, 1),
        tile_mask.transpose(0, 2, 1),
        assignment,
        metric_factor,
    )
    low, table = transform(True, 0, row_blocks // 2, n_basis, scalars, orbitals, b_tiles)
    (high,) = transform(False, row_blocks // 2, row_blocks // 2, n_basis, scalars, table, b_tiles)

    swap = [(0, 1), (1, 0)]
    ring = [(2 * i, 2 * ((i + 1) % n_aux)) for i in range(n_aux)]
    ring += [(2 * i + 1, 2 * ((i - 1) % n_aux) + 1) for i in range(n_aux)]

    def forward(slab):
        got = []
        for part in slab:
            got.append(lax.ppermute(part, ("aux", "occ"), ring))
        return tuple(got)

    def along(payload, links):
        pairs = []
        for i in range(n_aux):
            for c, sign in ((0, 1), (1, -1)):
                for ends in links:
                    at = [(i * n_orb + (i // per_orb + sign * k) % n_orb) * 2 + c for k in ends]
                    pairs.append(tuple(at))
        return lax.ppermute(payload, ("aux", "orb", "occ"), pairs)

    a = (low, high)
    b = []
    for part in a:
        b.append(lax.ppermute(part, "occ", swap))
    steps = n_aux // 2
    batches, batch, sends = [], [a], []
    for t in range(1, steps + 1):
        a = forward(a)
        batch.append(a)
        if t < steps:
            b = forward(b)
            batch.append(b)
        if t in BATCH_ENDS or t == steps:
            own = stage(batch, plane_rows)
            if t < steps:
                first = along(own, [(0, 1)])
                both = choose(own, first, plane_rows, mu_dev)
                sends.append((both, along(both, [(0, 3), (1, 2)])))
            else:
                sends.append((own, *(along(own, [(0, j)]) for j in range(1, n_orb))))
            batches.append(batch)
            batch = []

    partial = None
    for candidates, slabs in zip(sends, batches, strict=True):
        partial = accumulate(candidates, slabs, partial, block_rows, mu_dev)
    mine, other = partial
    return mine + lax.ppermute(other, "occ", swap)


def solution(mesh):
    in_specs = (
        P(("grp", "aux"), "orb", None, None, None),
        P(("grp", "aux"), "orb", None),
        P(("grp", "aux"), "orb", None),
        P(("grp", "aux")),
        P("grp"),
        P("grp", None),
        P(("grp", "occ")),
    )
    out_specs = P(("grp", "aux", "occ"), "orb")

    return jax.shard_map(
        per_device, mesh=mesh, in_specs=in_specs, out_specs=out_specs, check_vma=False
    )
```

time: 155 us -> 113 us (0.73)
  waiting for transfers between devices: 56.2 us -> 16.3 us
  Pallas kernels: 21.4 us -> 16.3 us
  starting transfers between devices: 73.3 us -> 78 us
    ppermute x32, waiting for transfers between devices: 45.6 us -> 13.9 us  [the longest x30 13.9 us: forward(): got.append(lax.ppermute(part, ('aux', 'occ'), ring))]
    ppermute x32, starting transfers between devices: 27.6 us -> 55.5 us  [the longest x30 34.8 us: forward(): got.append(lax.ppermute(part, ('aux', 'occ'), ring))]
    ppermute x11 -> x7, starting transfers between devices: 34.2 us -> 16.3 us  [along(): return lax.ppermute(payload, ('aux', 'orb', 'occ'), pairs)]
    ppermute x11 -> x7, waiting for transfers between devices: 9.13 us -> 0.91 us  [along(): return lax.ppermute(payload, ('aux', 'orb', 'occ'), pairs)]
    pallas_call x11 -> x8, Pallas kernels: 9.52 us -> 3.22 us  [the longest x3 3.03 us: accumulate(): pl.pallas_call(functools.partial(accumulate_kernel, len(candidates), coun...]
    ppermute x1, starting transfers between devices: 11.5 us -> 6.15 us  [per_device(): return mine + lax.ppermute(other, 'occ', swap)]
  transfers between devices with their start and end apart: 44 -> 40, of which waited for: 38 -> 11; matrix products, arithmetic and copies ran while one was open for 0% -> 0% of each run, Pallas kernels for 3% -> 2%
where the time goes in v2:
time: 113 us
  starting transfers between devices  78 us (69%)
  Pallas kernels  16.3 us (14%)
  waiting for transfers between devices  16.3 us (14%)
    ppermute x30, starting transfers between devices, forward(): got.append(lax.ppermute(part, ('aux', 'occ'), ring))  34.8 us
    ppermute x2, starting transfers between devices, per_device(): b.append(lax.ppermute(part, 'occ', swap))  20.7 us
    ppermute x7, starting transfers between devices, along(): return lax.ppermute(payload, ('aux', 'orb', 'occ'), pairs)  16.3 us
    ppermute x30, waiting for transfers between devices, forward(): got.append(lax.ppermute(part, ('aux', 'occ'), ring))  13.9 us
    pallas_call x2, Pallas kernels, transform(): pl.pallas_call(functools.partial(transform_kernel, build, n_basis, block0...  13.1 us
    ppermute x1, starting transfers between devices, per_device(): return mine + lax.ppermute(other, 'occ', swap)  6.15 us
    pallas_call x3, Pallas kernels, accumulate(): pl.pallas_call(functools.partial(accumulate_kernel, len(candidates), coun...  3.03 us
  transfers between devices with their start and end apart: 40, of which 11 were waited for; matrix products, arithmetic and copies ran while one was open for 0% of the time, Pallas kernels for 2%

profile of v2, /device:TPU:33, one launch (start us, length us, event | category | flops | bytes accessed | tf_op | source)
XLA Modules:
  0.0 112.7 jit_solution(16509006458025166502)
XLA Ops:
  0.0 7.5 %transform_first.1 = (bf16[512,128]{1,0:T(8,128)(2,1)}, bf16[4224,128]{1,0:T(8,128)(2,1)}) custom-call(s32[16]{0:T(128)} %index_ref.3, s32[8,4,8]{2,1,0:T(4,128)} %bitcast.2, s32[8,4,8]{2,1,0:T(4,128)} %bitcast.4, s32[8]{0:T(128)} %assign_ref.3, f32[128]{0:T(128)} %metric_ref.3, bf16[400,4000]{1,0:T(8,128)(2,1)} %table_or_orbitals_ref.1, ...), custom_call_target="tpu_custom_call" | custom-call | flops 536870912 | bytes 4194304 | tf_op jit(solution)/shard_map/transform_first/pallas_call | solution.py:129
  7.5 0.0 copy-start.2
  7.5 5.6 %transform_rest.1.refs_1_.refs_3_ = bf16[512,128]{1,0:T(8,128)(2,1)} custom-call(s32[16]{0:T(128)} %index_ref.3, s32[8,4,8]{2,1,0:T(4,128)} %bitcast.3, s32[8,4,8]{2,1,0:T(4,128)} %bitcast.5, s32[8]{0:T(128)} %assign_ref.3, f32[128]{0:T(128)} %metric_ref.3, bf16[4224,128]{1,0:T(8,128)(2,1)} %get-tuple-element.14.table_or_orbitals_ref, ...), custom_call_target="tpu_custom_call" | custom-call | flops 536870912 | bytes 4194304 | tf_op jit(solution)/shard_map/transform_rest/pallas_call | solution.py:129
  13.1 20.5 %collective-permute-start.22 = (bf16[512,128]{1,0:T(8,128)(2,1)}, bf16[512,128]{1,0:T(8,128)(2,1)S(1)}, u32[]{:S(2)}, u32[]{:S(2)}) collective-permute-start(bf16[512,128]{1,0:T(8,128)(2,1)} %transform_rest.1.refs_1_.refs_3_), channel_id=1, source_target_pairs={{0,1},{1,0},{2,3},{3,2},{4,5},{5,4},{6,7},{7,6},{8,9},{9,8},{10,11... | collective-permute-start | bytes 393224 | tf_op jit(solution)/shard_map/ppermute | solution.py:316
  33.7 0.2 collective-permute-start.14
  33.8 3.1 %collective-permute-start.7 = (bf16[512,128]{1,0:T(8,128)(2,1)}, bf16[512,128]{1,0:T(8,128)(2,1)S(1)}, u32[]{:S(2)}, u32[]{:S(2)}) collective-permute-start(bf16[512,128]{1,0:T(8,128)(2,1)} %transform_rest.1.refs_1_.refs_3_), channel_id=1, source_target_pairs={{0,8},{8,16},{16,24},{24,32},{32,40},{40,48},{48,56},{56,64},{64,7... | collective-permute-start | bytes 393224 | tf_op jit(solution)/shard_map/ppermute | solution.py:301
  36.9 0.0 collective-permute-start
  37.0 1.0 collective-permute-start.23
  38.0 0.0 collective-permute-done.14
  38.0 0.2 collective-permute-start.15
  38.1 1.0 collective-permute-done.7.refs_3_.refs_5_
  39.2 3.0 %collective-permute-start.8 = (bf16[512,128]{1,0:T(8,128)(2,1)S(1)}, bf16[512,128]{1,0:T(8,128)(2,1)S(1)}, u32[]{:S(2)}, u32[]{:S(2)}) collective-permute-start(bf16[512,128]{1,0:T(8,128)(2,1)S(1)} %collective-permute-done.7.refs_3_.refs_5_), channel_id=1, source_target_pairs={{0,8},{8,16},{16,24},{24,32},{32,40},{40,48},{48,56},{56,64},{64,7... | collective-permute-start | bytes 393224 | tf_op jit(solution)/shard_map/ppermute | solution.py:301
  42.2 0.0 collective-permute-done.refs_2_.refs_4_
  42.2 1.4 %collective-permute-start.1 = (bf16[512,128]{1,0:T(8,128)(2,1)S(1)}, bf16[512,128]{1,0:T(8,128)(2,1)S(1)}, u32[]{:S(2)}, u32[]{:S(2)}) collective-permute-start(bf16[512,128]{1,0:T(8,128)(2,1)S(1)} %collective-permute-done.refs_2_.refs_4_), channel_id=1, source_target_pairs={{0,8},{8,16},{16,24},{24,32},{32,40},{40,48},{48,56},{56,64},{64,7... | collective-permute-start | bytes 393224 | tf_op jit(solution)/shard_map/ppermute | solution.py:301
  43.6 1.4 %collective-permute-start.24 = (bf16[512,128]{1,0:T(8,128)(2,1)S(1)}, bf16[512,128]{1,0:T(8,128)(2,1)S(1)}, u32[]{:S(2)}, u32[]{:S(2)}) collective-permute-start(bf16[512,128]{1,0:T(8,128)(2,1)S(1)} %collective-permute-done.23.refs_5_.refs_7_), channel_id=1, source_target_pairs={{0,8},{8,16},{16,24},{24,32},{32,40},{40,48},{48,56},{56,64},{64,7... | collective-permute-start | bytes 393224 | tf_op jit(solution)/shard_map/ppermute | solution.py:301
  45.0 0.0 collective-permute-done.15.refs_4_.refs_6_
  45.0 1.4 %collective-permute-start.16 = (bf16[512,128]{1,0:T(8,128)(2,1)S(1)}, bf16[512,128]{1,0:T(8,128)(2,1)S(1)}, u32[]{:S(2)}, u32[]{:S(2)}) collective-permute-start(bf16[512,128]{1,0:T(8,128)(2,1)S(1)} %collective-permute-done.15.refs_4_.refs_6_), channel_id=1, source_target_pairs={{0,8},{8,16},{16,24},{24,32},{32,40},{40,48},{48,56},{56,64},{64,7... | collective-permute-start | bytes 393224 | tf_op jit(solution)/shard_map/ppermute | solution.py:301
  46.4 1.4 %collective-permute-start.9 = (bf16[512,128]{1,0:T(8,128)(2,1)S(1)}, bf16[512,128]{1,0:T(8,128)(2,1)S(1)}, u32[]{:S(2)}, u32[]{:S(2)}) collective-permute-start(bf16[512,128]{1,0:T(8,128)(2,1)S(1)} %collective-permute-done.8.refs_7_.refs_9_), channel_id=1, source_target_pairs={{0,8},{8,16},{16,24},{24,32},{32,40},{40,48},{48,56},{56,64},{64,7... | collective-permute-start | bytes 393224 | tf_op jit(solution)/shard_map/ppermute | solution.py:301
  47.8 1.4 %collective-permute-start.2 = (bf16[512,128]{1,0:T(8,128)(2,1)S(1)}, bf16[512,128]{1,0:T(8,128)(2,1)S(1)}, u32[]{:S(2)}, u32[]{:S(2)}) collective-permute-start(bf16[512,128]{1,0:T(8,128)(2,1)S(1)} %collective-permute-done.1.refs_6_.refs_8_), channel_id=1, source_target_pairs={{0,8},{8,16},{16,24},{24,32},{32,40},{40,48},{48,56},{56,64},{64,7... | collective-permute-start | bytes 393224 | tf_op jit(solution)/shard_map/ppermute | solution.py:301
  49.2 1.4 %collective-permute-start.25 = (bf16[512,128]{1,0:T(8,128)(2,1)S(1)}, bf16[512,128]{1,0:T(8,128)(2,1)S(1)}, u32[]{:S(2)}, u32[]{:S(2)}) collective-permute-start(bf16[512,128]{1,0:T(8,128)(2,1)S(1)} %collective-permute-done.24.refs_9_.refs_11_), channel_id=1, source_target_pairs={{0,8},{8,16},{16,24},{24,32},{32,40},{40,48},{48,56},{56,64},{64,7... | collective-permute-start | bytes 393224 | tf_op jit(solution)/shard_map/ppermute | solution.py:301
  50.6 1.4 %collective-permute-start.17 = (bf16[512,128]{1,0:T(8,128)(2,1)S(1)}, bf16[512,128]{1,0:T(8,128)(2,1)S(1)}, u32[]{:S(2)}, u32[]{:S(2)}) collective-permute-start(bf16[512,128]{1,0:T(8,128)(2,1)S(1)} %collective-permute-done.16.refs_8_.refs_10_), channel_id=1, source_target_pairs={{0,8},{8,16},{16,24},{24,32},{32,40},{40,48},{48,56},{56,64},{64,7... | collective-permute-start | bytes 393224 | tf_op jit(solution)/shard_map/ppermute | solution.py:301
  52.0 1.4 %collective-permute-start.10 = (bf16[512,128]{1,0:T(8,128)(2,1)S(1)}, bf16[512,128]{1,0:T(8,128)(2,1)S(1)}, u32[]{:S(2)}, u32[]{:S(2)}) collective-permute-start(bf16[512,128]{1,0:T(8,128)(2,1)S(1)} %collective-permute-done.9.refs_11_.refs_13_), channel_id=1, source_target_pairs={{0,8},{8,16},{16,24},{24,32},{32,40},{40,48},{48,56},{56,64},{64,7... | collective-permute-start | bytes 393224 | tf_op jit(solution)/shard_map/ppermute | solution.py:301
  53.4 1.4 %collective-permute-start.3 = (bf16[512,128]{1,0:T(8,128)(2,1)S(1)}, bf16[512,128]{1,0:T(8,128)(2,1)S(1)}, u32[]{:S(2)}, u32[]{:S(2)}) collective-permute-start(bf16[512,128]{1,0:T(8,128)(2,1)S(1)} %collective-permute-done.2.refs_10_.refs_12_), channel_id=1, source_target_pairs={{0,8},{8,16},{16,24},{24,32},{32,40},{40,48},{48,56},{56,64},{64,7... | collective-permute-start | bytes 393224 | tf_op jit(solution)/shard_map/ppermute | solution.py:301
  54.8 1.4 %collective-permute-start.26 = (bf16[512,128]{1,0:T(8,128)(2,1)S(1)}, bf16[512,128]{1,0:T(8,128)(2,1)S(1)}, u32[]{:S(2)}, u32[]{:S(2)}) collective-permute-start(bf16[512,128]{1,0:T(8,128)(2,1)S(1)} %collective-permute-done.25.refs_13_.refs_15_), channel_id=1, source_target_pairs={{0,8},{8,16},{16,24},{24,32},{32,40},{40,48},{48,56},{56,64},{64,7... | collective-permute-start | bytes 393224 | tf_op jit(solution)/shard_map/ppermute | solution.py:301
  56.2 1.4 %collective-permute-start.18 = (bf16[512,128]{1,0:T(8,128)(2,1)S(1)}, bf16[512,128]{1,0:T(8,128)(2,1)S(1)}, u32[]{:S(2)}, u32[]{:S(2)}) collective-permute-start(bf16[512,128]{1,0:T(8,128)(2,1)S(1)} %collective-permute-done.17.refs_12_.refs_14_), channel_id=1, source_target_pairs={{0,8},{8,16},{16,24},{24,32},{32,40},{40,48},{48,56},{56,64},{64,7... | collective-permute-start | bytes 393224 | tf_op jit(solution)/shard_map/ppermute | solution.py:301
  57.6 1.4 %collective-permute-start.11 = (bf16[512,128]{1,0:T(8,128)(2,1)S(1)}, bf16[512,128]{1,0:T(8,128)(2,1)S(1)}, u32[]{:S(2)}, u32[]{:S(2)}) collective-permute-start(bf16[512,128]{1,0:T(8,128)(2,1)S(1)} %collective-permute-done.10.refs_1_.refs_3_), channel_id=1, source_target_pairs={{0,8},{8,16},{16,24},{24,32},{32,40},{40,48},{48,56},{56,64},{64,7... | collective-permute-start | bytes 393224 | tf_op jit(solution)/shard_map/ppermute | solution.py:301
  59.0 1.4 %collective-permute-start.4 = (bf16[512,128]{1,0:T(8,128)(2,1)S(1)}, bf16[512,128]{1,0:T(8,128)(2,1)S(1)}, u32[]{:S(2)}, u32[]{:S(2)}) collective-permute-start(bf16[512,128]{1,0:T(8,128)(2,1)S(1)} %collective-permute-done.3.refs_0_.refs_2_), channel_id=1, source_target_pairs={{0,8},{8,16},{16,24},{24,32},{32,40},{40,48},{48,56},{56,64},{64,7... | collective-permute-start | bytes 393224 | tf_op jit(solution)/shard_map/ppermute | solution.py:301
  60.4 1.4 %collective-permute-start.27 = (bf16[512,128]{1,0:T(8,128)(2,1)S(1)}, bf16[512,128]{1,0:T(8,128)(2,1)S(1)}, u32[]{:S(2)}, u32[]{:S(2)}) collective-permute-start(bf16[512,128]{1,0:T(8,128)(2,1)S(1)} %collective-permute-done.26.refs_3_.refs_5_), channel_id=1, source_target_pairs={{0,8},{8,16},{16,24},{24,32},{32,40},{40,48},{48,56},{56,64},{64,7... | collective-permute-start | bytes 393224 | tf_op jit(solution)/shard_map/ppermute | solution.py:301
  61.8 1.4 %collective-permute-start.19 = (bf16[512,128]{1,0:T(8,128)(2,1)S(1)}, bf16[512,128]{1,0:T(8,128)(2,1)S(1)}, u32[]{:S(2)}, u32[]{:S(2)}) collective-permute-start(bf16[512,128]{1,0:T(8,128)(2,1)S(1)} %collective-permute-done.18.refs_2_.refs_4_), channel_id=1, source_target_pairs={{0,8},{8,16},{16,24},{24,32},{32,40},{40,48},{48,56},{56,64},{64,7... | collective-permute-start | bytes 393224 | tf_op jit(solution)/shard_map/ppermute | solution.py:301
  63.2 0.9 copy-done
  64.1 0.1 stage.5.own_ref
  64.2 5.0 %collective-permute-start.37 = (bf16[1792,128]{1,0:T(8,128)(2,1)S(1)}, bf16[1792,128]{1,0:T(8,128)(2,1)S(1)}, u32[]{:S(2)}, u32[]{:S(2)}) collective-permute-start(bf16[1792,128]{1,0:T(8,128)(2,1)S(1)} %stage.5.own_ref), channel_id=1, source_target_pairs={{0,2},{1,7},{8,10},{9,15},{16,18},{17,23},{24,26},{25,31},{34,36},... | collective-permute-start | bytes 1376264 | tf_op jit(solution)/shard_map/ppermute | solution.py:311
  69.2 0.1 collective-permute-start.12
  69.4 0.1 collective-permute-start.5
  69.5 0.1 collective-permute-start.28
  69.7 0.1 collective-permute-start.20
  69.8 3.6 %collective-permute-done.12.refs_9_.refs_11_ = bf16[512,128]{1,0:T(8,128)(2,1)S(1)} collective-permute-done((bf16[512,128]{1,0:T(8,128)(2,1)S(1)}, bf16[512,128]{1,0:T(8,128)(2,1)S(1)}, u32[]{:S(2)}, u32[]{:S(2)}) %collective-permute-start.12) | collective-permute-done | bytes 131104 | tf_op jit(solution)/shard_map/ppermute | solution.py:301
  73.4 1.4 %collective-permute-done.5.refs_8_.refs_10_ = bf16[512,128]{1,0:T(8,128)(2,1)S(1)} collective-permute-done((bf16[512,128]{1,0:T(8,128)(2,1)S(1)}, bf16[512,128]{1,0:T(8,128)(2,1)S(1)}, u32[]{:S(2)}, u32[]{:S(2)}) %collective-permute-start.5) | collective-permute-done | bytes 131104 | tf_op jit(solution)/shard_map/ppermute | solution.py:301
  74.8 1.4 %collective-permute-done.28.refs_11_.refs_13_ = bf16[512,128]{1,0:T(8,128)(2,1)S(1)} collective-permute-done((bf16[512,128]{1,0:T(8,128)(2,1)S(1)}, bf16[512,128]{1,0:T(8,128)(2,1)S(1)}, u32[]{:S(2)}, u32[]{:S(2)}) %collective-permute-start.28) | collective-permute-done | bytes 131104 | tf_op jit(solution)/shard_map/ppermute | solution.py:301
  76.3 1.4 %collective-permute-done.20.refs_10_.refs_12_ = bf16[512,128]{1,0:T(8,128)(2,1)S(1)} collective-permute-done((bf16[512,128]{1,0:T(8,128)(2,1)S(1)}, bf16[512,128]{1,0:T(8,128)(2,1)S(1)}, u32[]{:S(2)}, u32[]{:S(2)}) %collective-permute-start.20) | collective-permute-done | bytes 131104 | tf_op jit(solution)/shard_map/ppermute | solution.py:301
  77.7 0.1 stage.4.own_ref
  77.7 1.3 %collective-permute-start.35 = (bf16[1536,128]{1,0:T(8,128)(2,1)S(1)}, bf16[1536,128]{1,0:T(8,128)(2,1)S(1)}, u32[]{:S(2)}, u32[]{:S(2)}) collective-permute-start(bf16[1536,128]{1,0:T(8,128)(2,1)S(1)} %stage.4.own_ref), channel_id=1, source_target_pairs={{0,2},{1,7},{8,10},{9,15},{16,18},{17,23},{24,26},{25,31},{34,36},... | collective-permute-start | bytes 1179656 | tf_op jit(solution)/shard_map/ppermute | solution.py:311
  79.1 0.6 collective-permute-start.13
  79.7 1.3 %collective-permute-start.38 = (bf16[1792,128]{1,0:T(8,128)(2,1)S(1)}, bf16[1792,128]{1,0:T(8,128)(2,1)S(1)}, u32[]{:S(2)}, u32[]{:S(2)}) collective-permute-start(bf16[1792,128]{1,0:T(8,128)(2,1)S(1)} %choose.3.refs_0_), channel_id=1, source_target_pairs={{0,6},{2,4},{1,3},{7,5},{8,14},{10,12},{9,11},{15,13},{16,22},{18,... | collective-permute-start | bytes 1376264 | tf_op jit(solution)/shard_map/ppermute | solution.py:311
  81.0 0.1 collective-permute-start.6
  81.2 1.8 %collective-permute-done.13.refs_1_.refs_5_ = bf16[512,128]{1,0:T(8,128)(2,1)S(1)} collective-permute-done((bf16[512,128]{1,0:T(8,128)(2,1)S(1)}, bf16[512,128]{1,0:T(8,128)(2,1)S(1)}, u32[]{:S(2)}, u32[]{:S(2)}) %collective-permute-start.13) | collective-permute-done | bytes 131104 | tf_op jit(solution)/shard_map/ppermute | solution.py:301
  83.0 1.7 %collective-permute-start.31 = (bf16[512,128]{1,0:T(8,128)(2,1)S(1)}, bf16[512,128]{1,0:T(8,128)(2,1)S(1)}, u32[]{:S(2)}, u32[]{:S(2)}) collective-permute-start(bf16[512,128]{1,0:T(8,128)(2,1)S(1)} %collective-permute-done.13.refs_1_.refs_5_), channel_id=1, source_target_pairs={{0,8},{8,16},{16,24},{24,32},{32,40},{40,48},{48,56},{56,64},{64,7... | collective-permute-start | bytes 393224 | tf_op jit(solution)/shard_map/ppermute | solution.py:301
  84.7 1.3 %collective-permute-start.36 = (bf16[1536,128]{1,0:T(8,128)(2,1)S(1)}, bf16[1536,128]{1,0:T(8,128)(2,1)S(1)}, u32[]{:S(2)}, u32[]{:S(2)}) collective-permute-start(bf16[1536,128]{1,0:T(8,128)(2,1)S(1)} %choose.2.refs_0_), channel_id=1, source_target_pairs={{0,6},{2,4},{1,3},{7,5},{8,14},{10,12},{9,11},{15,13},{16,22},{18,... | collective-permute-start | bytes 1179656 | tf_op jit(solution)/shard_map/ppermute | solution.py:311
  86.0 0.1 collective-permute-start.29
  86.2 0.3 collective-permute-start.30
  86.5 0.3 collective-permute-done.31.refs_5_.refs_9_
  86.8 3.2 %collective-permute-start.21 = (bf16[512,128]{1,0:T(8,128)(2,1)S(1)}, bf16[512,128]{1,0:T(8,128)(2,1)S(1)}, u32[]{:S(2)}, u32[]{:S(2)}) collective-permute-start(bf16[512,128]{1,0:T(8,128)(2,1)S(1)} %collective-permute-done.20.refs_10_.refs_12_), channel_id=1, source_target_pairs={{0,8},{8,16},{16,24},{24,32},{32,40},{40,48},{48,56},{56,64},{64,7... | collective-permute-start | bytes 393224 | tf_op jit(solution)/shard_map/ppermute | solution.py:301
  90.0 1.7 %collective-permute-done.30.refs_4_.refs_8_ = bf16[512,128]{1,0:T(8,128)(2,1)S(1)} collective-permute-done((bf16[512,128]{1,0:T(8,128)(2,1)S(1)}, bf16[512,128]{1,0:T(8,128)(2,1)S(1)}, u32[]{:S(2)}, u32[]{:S(2)}) %collective-permute-start.30) | collective-permute-done | bytes 131104 | tf_op jit(solution)/shard_map/ppermute | solution.py:301
  91.7 1.1 collective-permute-done.21.refs_2_.refs_6_
  92.8 4.7 %collective-permute-start.32 = (bf16[768,128]{1,0:T(8,128)(2,1)S(1)}, bf16[768,128]{1,0:T(8,128)(2,1)S(1)}, u32[]{:S(2)}, u32[]{:S(2)}) collective-permute-start(bf16[768,128]{1,0:T(8,128)(2,1)S(1)} %stage.3.refs_0_), channel_id=1, source_target_pairs={{0,2},{1,7},{8,10},{9,15},{16,18},{17,23},{24,26},{25,31},{34,36},... | collective-permute-start | bytes 589832 | tf_op jit(solution)/shard_map/ppermute | solution.py:311
  97.5 1.3 %collective-permute-start.33 = (bf16[768,128]{1,0:T(8,128)(2,1)S(1)}, bf16[768,128]{1,0:T(8,128)(2,1)S(1)}, u32[]{:S(2)}, u32[]{:S(2)}) collective-permute-start(bf16[768,128]{1,0:T(8,128)(2,1)S(1)} %stage.3.refs_0_), channel_id=1, source_target_pairs={{0,4},{1,5},{8,12},{9,13},{16,20},{17,21},{24,28},{25,29},{34,38},... | collective-permute-start | bytes 589832 | tf_op jit(solution)/shard_map/ppermute | solution.py:311
  98.9 1.3 %collective-permute-start.34 = (bf16[768,128]{1,0:T(8,128)(2,1)S(1)}, bf16[768,128]{1,0:T(8,128)(2,1)S(1)}, u32[]{:S(2)}, u32[]{:S(2)}) collective-permute-start(bf16[768,128]{1,0:T(8,128)(2,1)S(1)} %stage.3.refs_0_), channel_id=1, source_target_pairs={{0,6},{1,3},{8,14},{9,11},{16,22},{17,19},{24,30},{25,27},{34,32},... | collective-permute-start | bytes 589832 | tf_op jit(solution)/shard_map/ppermute | solution.py:311
  100.2 1.3 %accumulate.3 = (f32[128,1024]{1,0:T(8,128)S(1)}, f32[128,1024]{1,0:T(8,128)S(1)}) custom-call(bf16[1792,128]{1,0:T(8,128)(2,1)S(1)} %choose.3.refs_0_, bf16[1792,128]{1,0:T(8,128)(2,1)S(1)} %collective-permute-done.38.refs_1_, bf16[512,128]{1,0:T(8,128)(2,1)S(1)} %copy-done.2, bf16[512,128]{1,0:T(8,128)(2,1)S(1)} %copy-done.1, ...), custom_call_target="tpu_custom_call" | custom-call | flops 469762048 | tf_op jit(solution)/shard_map/accumulate/pallas_call | solution.py:263
  101.5 1.1 accumulate.4
  102.6 0.9 collective-permute-done.34.refs_3_
  103.5 0.6 accumulate.5
  104.2 6.2 %collective-permute-start.39 = (f32[128,1024]{1,0:T(8,128)S(1)}, f32[128,1024]{1,0:T(8,128)S(1)}, u32[]{:S(2)}, u32[]{:S(2)}) collective-permute-start(f32[128,1024]{1,0:T(8,128)S(1)} %get-tuple-element.20), channel_id=1, source_target_pairs={{0,1},{1,0},{2,3},{3,2},{4,5},{5,4},{6,7},{7,6},{8,9},{9,8},{10,11... | collective-permute-start | bytes 1572872 | tf_op jit(solution)/shard_map/ppermute | solution.py:340
  110.3 1.5 %collective-permute-done.39 = f32[128,1024]{1,0:T(8,128)S(1)} collective-permute-done((f32[128,1024]{1,0:T(8,128)S(1)}, f32[128,1024]{1,0:T(8,128)S(1)}, u32[]{:S(2)}, u32[]{:S(2)}) %collective-permute-start.39) | collective-permute-done | bytes 524320 | tf_op jit(solution)/shard_map/ppermute | solution.py:340
  111.9 0.9 add.3
  (33 shorter events, 0.2 us)
Async XLA Ops:
  7.5 26.1 %copy-start.2 = (bf16[512,128]{1,0:T(8,128)(2,1)S(1)}, bf16[512,128]{1,0:T(8,128)(2,1)}, u32[]{:S(2)}) copy-start(bf16[512,128]{1,0:T(8,128)(2,1)} %get-tuple-element.13.refs_0_.refs_2_) | copy-start | bytes 393220
  13.1 23.8 %collective-permute-start.22 = (bf16[512,128]{1,0:T(8,128)(2,1)}, bf16[512,128]{1,0:T(8,128)(2,1)S(1)}, u32[]{:S(2)}, u32[]{:S(2)}) collective-permute-start(bf16[512,128]{1,0:T(8,128)(2,1)} %transform_rest.1.refs_1_.refs_3_), channel_id=1, source_target_pairs={{0,1},{1,0},{2,3},{3,2},{4,5},{5,4},{6,7},{7,6},{8,9},{9,8},{10,11... | collective-permute-start | bytes 393224 | tf_op jit(solution)/shard_map/ppermute | solution.py:316
  33.7 4.3 %collective-permute-start.14 = (bf16[512,128]{1,0:T(8,128)(2,1)S(1)}, bf16[512,128]{1,0:T(8,128)(2,1)S(1)}, u32[]{:S(2)}, u32[]{:S(2)}) collective-permute-start(bf16[512,128]{1,0:T(8,128)(2,1)S(1)} %copy-done.2), channel_id=1, source_target_pairs={{0,1},{1,0},{2,3},{3,2},{4,5},{5,4},{6,7},{7,6},{8,9},{9,8},{10,11... | collective-permute-start | bytes 393224 | tf_op jit(solution)/shard_map/ppermute | solution.py:316
  33.8 5.4 %collective-permute-start.7 = (bf16[512,128]{1,0:T(8,128)(2,1)}, bf16[512,128]{1,0:T(8,128)(2,1)S(1)}, u32[]{:S(2)}, u32[]{:S(2)}) collective-permute-start(bf16[512,128]{1,0:T(8,128)(2,1)} %transform_rest.1.refs_1_.refs_3_), channel_id=1, source_target_pairs={{0,8},{8,16},{16,24},{24,32},{32,40},{40,48},{48,56},{56,64},{64,7... | collective-permute-start | bytes 393224 | tf_op jit(solution)/shard_map/ppermute | solution.py:301
  36.9 5.2 %collective-permute-start = (bf16[512,128]{1,0:T(8,128)(2,1)S(1)}, bf16[512,128]{1,0:T(8,128)(2,1)S(1)}, u32[]{:S(2)}, u32[]{:S(2)}) collective-permute-start(bf16[512,128]{1,0:T(8,128)(2,1)S(1)} %copy-done.2), channel_id=1, source_target_pairs={{0,8},{8,16},{16,24},{24,32},{32,40},{40,48},{48,56},{56,64},{64,7... | collective-permute-start | bytes 393224 | tf_op jit(solution)/shard_map/ppermute | solution.py:301
  37.0 6.6 %collective-permute-start.23 = (bf16[512,128]{1,0:T(8,128)(2,1)S(1)}, bf16[512,128]{1,0:T(8,128)(2,1)S(1)}, u32[]{:S(2)}, u32[]{:S(2)}) collective-permute-start(bf16[512,128]{1,0:T(8,128)(2,1)S(1)} %collective-permute-done.22), channel_id=1, source_target_pairs={{0,8},{8,16},{16,24},{24,32},{32,40},{40,48},{48,56},{56,64},{64,7... | collective-permute-start | bytes 393224 | tf_op jit(solution)/shard_map/ppermute | solution.py:301
  38.0 7.0 %collective-permute-start.15 = (bf16[512,128]{1,0:T(8,128)(2,1)S(1)}, bf16[512,128]{1,0:T(8,128)(2,1)S(1)}, u32[]{:S(2)}, u32[]{:S(2)}) collective-permute-start(bf16[512,128]{1,0:T(8,128)(2,1)S(1)} %collective-permute-done.14), channel_id=1, source_target_pairs={{0,8},{8,16},{16,24},{24,32},{32,40},{40,48},{48,56},{56,64},{64,7... | collective-permute-start | bytes 393224 | tf_op jit(solution)/shard_map/ppermute | solution.py:301
  39.2 7.2 %collective-permute-start.8 = (bf16[512,128]{1,0:T(8,128)(2,1)S(1)}, bf16[512,128]{1,0:T(8,128)(2,1)S(1)}, u32[]{:S(2)}, u32[]{:S(2)}) collective-permute-start(bf16[512,128]{1,0:T(8,128)(2,1)S(1)} %collective-permute-done.7.refs_3_.refs_5_), channel_id=1, source_target_pairs={{0,8},{8,16},{16,24},{24,32},{32,40},{40,48},{48,56},{56,64},{64,7... | collective-permute-start | bytes 393224 | tf_op jit(solution)/shard_map/ppermute | solution.py:301
  42.2 5.6 %collective-permute-start.1 = (bf16[512,128]{1,0:T(8,128)(2,1)S(1)}, bf16[512,128]{1,0:T(8,128)(2,1)S(1)}, u32[]{:S(2)}, u32[]{:S(2)}) collective-permute-start(bf16[512,128]{1,0:T(8,128)(2,1)S(1)} %collective-permute-done.refs_2_.refs_4_), channel_id=1, source_target_pairs={{0,8},{8,16},{16,24},{24,32},{32,40},{40,48},{48,56},{56,64},{64,7... | collective-permute-start | bytes 393224 | tf_op jit(solution)/shard_map/ppermute | solution.py:301
  43.6 5.6 %collective-permute-start.24 = (bf16[512,128]{1,0:T(8,128)(2,1)S(1)}, bf16[512,128]{1,0:T(8,128)(2,1)S(1)}, u32[]{:S(2)}, u32[]{:S(2)}) collective-permute-start(bf16[512,128]{1,0:T(8,128)(2,1)S(1)} %collective-permute-done.23.refs_5_.refs_7_), channel_id=1, source_target_pairs={{0,8},{8,16},{16,24},{24,32},{32,40},{40,48},{48,56},{56,64},{64,7... | collective-permute-start | bytes 393224 | tf_op jit(solution)/shard_map/ppermute | solution.py:301
  45.0 5.6 %collective-permute-start.16 = (bf16[512,128]{1,0:T(8,128)(2,1)S(1)}, bf16[512,128]{1,0:T(8,128)(2,1)S(1)}, u32[]{:S(2)}, u32[]{:S(2)}) collective-permute-start(bf16[512,128]{1,0:T(8,128)(2,1)S(1)} %collective-permute-done.15.refs_4_.refs_6_), channel_id=1, source_target_pairs={{0,8},{8,16},{16,24},{24,32},{32,40},{40,48},{48,56},{56,64},{64,7... | collective-permute-start | bytes 393224 | tf_op jit(solution)/shard_map/ppermute | solution.py:301
  46.4 5.6 %collective-permute-start.9 = (bf16[512,128]{1,0:T(8,128)(2,1)S(1)}, bf16[512,128]{1,0:T(8,128)(2,1)S(1)}, u32[]{:S(2)}, u32[]{:S(2)}) collective-permute-start(bf16[512,128]{1,0:T(8,128)(2,1)S(1)} %collective-permute-done.8.refs_7_.refs_9_), channel_id=1, source_target_pairs={{0,8},{8,16},{16,24},{24,32},{32,40},{40,48},{48,56},{56,64},{64,7... | collective-permute-start | bytes 393224 | tf_op jit(solution)/shard_map/ppermute | solution.py:301
  47.8 5.6 %collective-permute-start.2 = (bf16[512,128]{1,0:T(8,128)(2,1)S(1)}, bf16[512,128]{1,0:T(8,128)(2,1)S(1)}, u32[]{:S(2)}, u32[]{:S(2)}) collective-permute-start(bf16[512,128]{1,0:T(8,128)(2,1)S(1)} %collective-permute-done.1.refs_6_.refs_8_), channel_id=1, source_target_pairs={{0,8},{8,16},{16,24},{24,32},{32,40},{40,48},{48,56},{56,64},{64,7... | collective-permute-start | bytes 393224 | tf_op jit(solution)/shard_map/ppermute | solution.py:301
  49.2 5.6 %collective-permute-start.25 = (bf16[512,128]{1,0:T(8,128)(2,1)S(1)}, bf16[512,128]{1,0:T(8,128)(2,1)S(1)}, u32[]{:S(2)}, u32[]{:S(2)}) collective-permute-start(bf16[512,128]{1,0:T(8,128)(2,1)S(1)} %collective-permute-done.24.refs_9_.refs_11_), channel_id=1, source_target_pairs={{0,8},{8,16},{16,24},{24,32},{32,40},{40,48},{48,56},{56,64},{64,7... | collective-permute-start | bytes 393224 | tf_op jit(solution)/shard_map/ppermute | solution.py:301
  50.6 5.6 %collective-permute-start.17 = (bf16[512,128]{1,0:T(8,128)(2,1)S(1)}, bf16[512,128]{1,0:T(8,128)(2,1)S(1)}, u32[]{:S(2)}, u32[]{:S(2)}) collective-permute-start(bf16[512,128]{1,0:T(8,128)(2,1)S(1)} %collective-permute-done.16.refs_8_.refs_10_), channel_id=1, source_target_pairs={{0,8},{8,16},{16,24},{24,32},{32,40},{40,48},{48,56},{56,64},{64,7... | collective-permute-start | bytes 393224 | tf_op jit(solution)/shard_map/ppermute | solution.py:301
  52.0 5.6 %collective-permute-start.10 = (bf16[512,128]{1,0:T(8,128)(2,1)S(1)}, bf16[512,128]{1,0:T(8,128)(2,1)S(1)}, u32[]{:S(2)}, u32[]{:S(2)}) collective-permute-start(bf16[512,128]{1,0:T(8,128)(2,1)S(1)} %collective-permute-done.9.refs_11_.refs_13_), channel_id=1, source_target_pairs={{0,8},{8,16},{16,24},{24,32},{32,40},{40,48},{48,56},{56,64},{64,7... | collective-permute-start | bytes 393224 | tf_op jit(solution)/shard_map/ppermute | solution.py:301
  53.4 5.6 %collective-permute-start.3 = (bf16[512,128]{1,0:T(8,128)(2,1)S(1)}, bf16[512,128]{1,0:T(8,128)(2,1)S(1)}, u32[]{:S(2)}, u32[]{:S(2)}) collective-permute-start(bf16[512,128]{1,0:T(8,128)(2,1)S(1)} %collective-permute-done.2.refs_10_.refs_12_), channel_id=1, source_target_pairs={{0,8},{8,16},{16,24},{24,32},{32,40},{40,48},{48,56},{56,64},{64,7... | collective-permute-start | bytes 393224 | tf_op jit(solution)/shard_map/ppermute | solution.py:301
  54.8 5.6 %collective-permute-start.26 = (bf16[512,128]{1,0:T(8,128)(2,1)S(1)}, bf16[512,128]{1,0:T(8,128)(2,1)S(1)}, u32[]{:S(2)}, u32[]{:S(2)}) collective-permute-start(bf16[512,128]{1,0:T(8,128)(2,1)S(1)} %collective-permute-done.25.refs_13_.refs_15_), channel_id=1, source_target_pairs={{0,8},{8,16},{16,24},{24,32},{32,40},{40,48},{48,56},{56,64},{64,7... | collective-permute-start | bytes 393224 | tf_op jit(solution)/shard_map/ppermute | solution.py:301
  56.2 5.6 %collective-permute-start.18 = (bf16[512,128]{1,0:T(8,128)(2,1)S(1)}, bf16[512,128]{1,0:T(8,128)(2,1)S(1)}, u32[]{:S(2)}, u32[]{:S(2)}) collective-permute-start(bf16[512,128]{1,0:T(8,128)(2,1)S(1)} %collective-permute-done.17.refs_12_.refs_14_), channel_id=1, source_target_pairs={{0,8},{8,16},{16,24},{24,32},{32,40},{40,48},{48,56},{56,64},{64,7... | collective-permute-start | bytes 393224 | tf_op jit(solution)/shard_map/ppermute | solution.py:301
  57.6 11.6 %collective-permute-start.11 = (bf16[512,128]{1,0:T(8,128)(2,1)S(1)}, bf16[512,128]{1,0:T(8,128)(2,1)S(1)}, u32[]{:S(2)}, u32[]{:S(2)}) collective-permute-start(bf16[512,128]{1,0:T(8,128)(2,1)S(1)} %collective-permute-done.10.refs_1_.refs_3_), channel_id=1, source_target_pairs={{0,8},{8,16},{16,24},{24,32},{32,40},{40,48},{48,56},{56,64},{64,7... | collective-permute-start | bytes 393224 | tf_op jit(solution)/shard_map/ppermute | solution.py:301
  59.0 10.3 %collective-permute-start.4 = (bf16[512,128]{1,0:T(8,128)(2,1)S(1)}, bf16[512,128]{1,0:T(8,128)(2,1)S(1)}, u32[]{:S(2)}, u32[]{:S(2)}) collective-permute-start(bf16[512,128]{1,0:T(8,128)(2,1)S(1)} %collective-permute-done.3.refs_0_.refs_2_), channel_id=1, source_target_pairs={{0,8},{8,16},{16,24},{24,32},{32,40},{40,48},{48,56},{56,64},{64,7... | collective-permute-start | bytes 393224 | tf_op jit(solution)/shard_map/ppermute | solution.py:301
  60.4 9.1 %collective-permute-start.27 = (bf16[512,128]{1,0:T(8,128)(2,1)S(1)}, bf16[512,128]{1,0:T(8,128)(2,1)S(1)}, u32[]{:S(2)}, u32[]{:S(2)}) collective-permute-start(bf16[512,128]{1,0:T(8,128)(2,1)S(1)} %collective-permute-done.26.refs_3_.refs_5_), channel_id=1, source_target_pairs={{0,8},{8,16},{16,24},{24,32},{32,40},{40,48},{48,56},{56,64},{64,7... | collective-permute-start | bytes 393224 | tf_op jit(solution)/shard_map/ppermute | solution.py:301
  61.8 7.8 %collective-permute-start.19 = (bf16[512,128]{1,0:T(8,128)(2,1)S(1)}, bf16[512,128]{1,0:T(8,128)(2,1)S(1)}, u32[]{:S(2)}, u32[]{:S(2)}) collective-permute-start(bf16[512,128]{1,0:T(8,128)(2,1)S(1)} %collective-permute-done.18.refs_2_.refs_4_), channel_id=1, source_target_pairs={{0,8},{8,16},{16,24},{24,32},{32,40},{40,48},{48,56},{56,64},{64,7... | collective-permute-start | bytes 393224 | tf_op jit(solution)/shard_map/ppermute | solution.py:301
  63.2 0.9 copy-start
  64.2 36.0 %copy-start.1 = (bf16[512,128]{1,0:T(8,128)(2,1)S(1)}, bf16[512,128]{1,0:T(8,128)(2,1)}, u32[]{:S(2)}) copy-start(bf16[512,128]{1,0:T(8,128)(2,1)} %transform_rest.1.refs_1_.refs_3_) | copy-start | bytes 393220
  64.2 15.4 %collective-permute-start.37 = (bf16[1792,128]{1,0:T(8,128)(2,1)S(1)}, bf16[1792,128]{1,0:T(8,128)(2,1)S(1)}, u32[]{:S(2)}, u32[]{:S(2)}) collective-permute-start(bf16[1792,128]{1,0:T(8,128)(2,1)S(1)} %stage.5.own_ref), channel_id=1, source_target_pairs={{0,2},{1,7},{8,10},{9,15},{16,18},{17,23},{24,26},{25,31},{34,36},... | collective-permute-start | bytes 1376264 | tf_op jit(solution)/shard_map/ppermute | solution.py:311
  69.2 4.2 %collective-permute-start.12 = (bf16[512,128]{1,0:T(8,128)(2,1)S(1)}, bf16[512,128]{1,0:T(8,128)(2,1)S(1)}, u32[]{:S(2)}, u32[]{:S(2)}) collective-permute-start(bf16[512,128]{1,0:T(8,128)(2,1)S(1)} %collective-permute-done.11.refs_5_.refs_7_), channel_id=1, source_target_pairs={{0,8},{8,16},{16,24},{24,32},{32,40},{40,48},{48,56},{56,64},{64,7... | collective-permute-start | bytes 393224 | tf_op jit(solution)/shard_map/ppermute | solution.py:301
  69.4 5.5 %collective-permute-start.5 = (bf16[512,128]{1,0:T(8,128)(2,1)S(1)}, bf16[512,128]{1,0:T(8,128)(2,1)S(1)}, u32[]{:S(2)}, u32[]{:S(2)}) collective-permute-start(bf16[512,128]{1,0:T(8,128)(2,1)S(1)} %collective-permute-done.4.refs_4_.refs_6_), channel_id=1, source_target_pairs={{0,8},{8,16},{16,24},{24,32},{32,40},{40,48},{48,56},{56,64},{64,7... | collective-permute-start | bytes 393224 | tf_op jit(solution)/shard_map/ppermute | solution.py:301
  69.5 6.7 %collective-permute-start.28 = (bf16[512,128]{1,0:T(8,128)(2,1)S(1)}, bf16[512,128]{1,0:T(8,128)(2,1)S(1)}, u32[]{:S(2)}, u32[]{:S(2)}) collective-permute-start(bf16[512,128]{1,0:T(8,128)(2,1)S(1)} %collective-permute-done.27.refs_7_.refs_9_), channel_id=1, source_target_pairs={{0,8},{8,16},{16,24},{24,32},{32,40},{40,48},{48,56},{56,64},{64,7... | collective-permute-start | bytes 393224 | tf_op jit(solution)/shard_map/ppermute | solution.py:301
  69.7 8.0 %collective-permute-start.20 = (bf16[512,128]{1,0:T(8,128)(2,1)S(1)}, bf16[512,128]{1,0:T(8,128)(2,1)S(1)}, u32[]{:S(2)}, u32[]{:S(2)}) collective-permute-start(bf16[512,128]{1,0:T(8,128)(2,1)S(1)} %collective-permute-done.19.refs_6_.refs_8_), channel_id=1, source_target_pairs={{0,8},{8,16},{16,24},{24,32},{32,40},{40,48},{48,56},{56,64},{64,7... | collective-permute-start | bytes 393224 | tf_op jit(solution)/shard_map/ppermute | solution.py:301
  77.7 6.9 %collective-permute-start.35 = (bf16[1536,128]{1,0:T(8,128)(2,1)S(1)}, bf16[1536,128]{1,0:T(8,128)(2,1)S(1)}, u32[]{:S(2)}, u32[]{:S(2)}) collective-permute-start(bf16[1536,128]{1,0:T(8,128)(2,1)S(1)} %stage.4.own_ref), channel_id=1, source_target_pairs={{0,2},{1,7},{8,10},{9,15},{16,18},{17,23},{24,26},{25,31},{34,36},... | collective-permute-start | bytes 1179656 | tf_op jit(solution)/shard_map/ppermute | solution.py:311
  79.1 3.9 %collective-permute-start.13 = (bf16[512,128]{1,0:T(8,128)(2,1)S(1)}, bf16[512,128]{1,0:T(8,128)(2,1)S(1)}, u32[]{:S(2)}, u32[]{:S(2)}) collective-permute-start(bf16[512,128]{1,0:T(8,128)(2,1)S(1)} %collective-permute-done.12.refs_9_.refs_11_), channel_id=1, source_target_pairs={{0,8},{8,16},{16,24},{24,32},{32,40},{40,48},{48,56},{56,64},{64,7... | collective-permute-start | bytes 393224 | tf_op jit(solution)/shard_map/ppermute | solution.py:301
  79.7 20.5 %collective-permute-start.38 = (bf16[1792,128]{1,0:T(8,128)(2,1)S(1)}, bf16[1792,128]{1,0:T(8,128)(2,1)S(1)}, u32[]{:S(2)}, u32[]{:S(2)}) collective-permute-start(bf16[1792,128]{1,0:T(8,128)(2,1)S(1)} %choose.3.refs_0_), channel_id=1, source_target_pairs={{0,6},{2,4},{1,3},{7,5},{8,14},{10,12},{9,11},{15,13},{16,22},{18,... | collective-permute-start | bytes 1376264 | tf_op jit(solution)/shard_map/ppermute | solution.py:311
  81.0 5.2 %collective-permute-start.6 = (bf16[512,128]{1,0:T(8,128)(2,1)S(1)}, bf16[512,128]{1,0:T(8,128)(2,1)S(1)}, u32[]{:S(2)}, u32[]{:S(2)}) collective-permute-start(bf16[512,128]{1,0:T(8,128)(2,1)S(1)} %collective-permute-done.5.refs_8_.refs_10_), channel_id=1, source_target_pairs={{0,8},{8,16},{16,24},{24,32},{32,40},{40,48},{48,56},{56,64},{64,7... | collective-permute-start | bytes 393224 | tf_op jit(solution)/shard_map/ppermute | solution.py:301
  83.0 3.8 %collective-permute-start.31 = (bf16[512,128]{1,0:T(8,128)(2,1)S(1)}, bf16[512,128]{1,0:T(8,128)(2,1)S(1)}, u32[]{:S(2)}, u32[]{:S(2)}) collective-permute-start(bf16[512,128]{1,0:T(8,128)(2,1)S(1)} %collective-permute-done.13.refs_1_.refs_5_), channel_id=1, source_target_pairs={{0,8},{8,16},{16,24},{24,32},{32,40},{40,48},{48,56},{56,64},{64,7... | collective-permute-start | bytes 393224 | tf_op jit(solution)/shard_map/ppermute | solution.py:301
  84.7 16.8 %collective-permute-start.36 = (bf16[1536,128]{1,0:T(8,128)(2,1)S(1)}, bf16[1536,128]{1,0:T(8,128)(2,1)S(1)}, u32[]{:S(2)}, u32[]{:S(2)}) collective-permute-start(bf16[1536,128]{1,0:T(8,128)(2,1)S(1)} %choose.2.refs_0_), channel_id=1, source_target_pairs={{0,6},{2,4},{1,3},{7,5},{8,14},{10,12},{9,11},{15,13},{16,22},{18,... | collective-permute-start | bytes 1179656 | tf_op jit(solution)/shard_map/ppermute | solution.py:311
  86.0 4.0 %collective-permute-start.29 = (bf16[512,128]{1,0:T(8,128)(2,1)S(1)}, bf16[512,128]{1,0:T(8,128)(2,1)S(1)}, u32[]{:S(2)}, u32[]{:S(2)}) collective-permute-start(bf16[512,128]{1,0:T(8,128)(2,1)S(1)} %collective-permute-done.28.refs_11_.refs_13_), channel_id=1, source_target_pairs={{0,8},{8,16},{16,24},{24,32},{32,40},{40,48},{48,56},{56,64},{64,7... | collective-permute-start | bytes 393224 | tf_op jit(solution)/shard_map/ppermute | solution.py:301
  86.2 5.5 %collective-permute-start.30 = (bf16[512,128]{1,0:T(8,128)(2,1)S(1)}, bf16[512,128]{1,0:T(8,128)(2,1)S(1)}, u32[]{:S(2)}, u32[]{:S(2)}) collective-permute-start(bf16[512,128]{1,0:T(8,128)(2,1)S(1)} %collective-permute-done.6.refs_0_.refs_4_), channel_id=1, source_target_pairs={{0,8},{8,16},{16,24},{24,32},{32,40},{40,48},{48,56},{56,64},{64,7... | collective-permute-start | bytes 393224 | tf_op jit(solution)/shard_map/ppermute | solution.py:301
  86.8 6.0 %collective-permute-start.21 = (bf16[512,128]{1,0:T(8,128)(2,1)S(1)}, bf16[512,128]{1,0:T(8,128)(2,1)S(1)}, u32[]{:S(2)}, u32[]{:S(2)}) collective-permute-start(bf16[512,128]{1,0:T(8,128)(2,1)S(1)} %collective-permute-done.20.refs_10_.refs_12_), channel_id=1, source_target_pairs={{0,8},{8,16},{16,24},{24,32},{32,40},{40,48},{48,56},{56,64},{64,7... | collective-permute-start | bytes 393224 | tf_op jit(solution)/shard_map/ppermute | solution.py:301
  92.8 9.8 %collective-permute-start.32 = (bf16[768,128]{1,0:T(8,128)(2,1)S(1)}, bf16[768,128]{1,0:T(8,128)(2,1)S(1)}, u32[]{:S(2)}, u32[]{:S(2)}) collective-permute-start(bf16[768,128]{1,0:T(8,128)(2,1)S(1)} %stage.3.refs_0_), channel_id=1, source_target_pairs={{0,2},{1,7},{8,10},{9,15},{16,18},{17,23},{24,26},{25,31},{34,36},... | collective-permute-start | bytes 589832 | tf_op jit(solution)/shard_map/ppermute | solution.py:311
  97.5 5.1 %collective-permute-start.33 = (bf16[768,128]{1,0:T(8,128)(2,1)S(1)}, bf16[768,128]{1,0:T(8,128)(2,1)S(1)}, u32[]{:S(2)}, u32[]{:S(2)}) collective-permute-start(bf16[768,128]{1,0:T(8,128)(2,1)S(1)} %stage.3.refs_0_), channel_id=1, source_target_pairs={{0,4},{1,5},{8,12},{9,13},{16,20},{17,21},{24,28},{25,29},{34,38},... | collective-permute-start | bytes 589832 | tf_op jit(solution)/shard_map/ppermute | solution.py:311
  98.9 4.7 %collective-permute-start.34 = (bf16[768,128]{1,0:T(8,128)(2,1)S(1)}, bf16[768,128]{1,0:T(8,128)(2,1)S(1)}, u32[]{:S(2)}, u32[]{:S(2)}) collective-permute-start(bf16[768,128]{1,0:T(8,128)(2,1)S(1)} %stage.3.refs_0_), channel_id=1, source_target_pairs={{0,6},{1,3},{8,14},{9,11},{16,22},{17,19},{24,30},{25,27},{34,32},... | collective-permute-start | bytes 589832 | tf_op jit(solution)/shard_map/ppermute | solution.py:311
  104.2 7.7 %collective-permute-start.39 = (f32[128,1024]{1,0:T(8,128)S(1)}, f32[128,1024]{1,0:T(8,128)S(1)}, u32[]{:S(2)}, u32[]{:S(2)}) collective-permute-start(f32[128,1024]{1,0:T(8,128)S(1)} %get-tuple-element.20), channel_id=1, source_target_pairs={{0,1},{1,0},{2,3},{3,2},{4,5},{5,4},{6,7},{7,6},{8,9},{9,8},{10,11... | collective-permute-start | bytes 1572872 | tf_op jit(solution)/shard_map/ppermute | solution.py:340
